TPU v7x, 8 devices: a whole 2x2x1 slice. The times are simulated.
8 devices in a mesh: ep: 8 (over z, y, x, core).
Axes of the slice: x: 2, y: 2, z: 1, core: 2. Of those that a mesh axis runs over, the one named last changes fastest.
Arguments:
- tokens: bfloat16 [4096, 512], P('ep')
- grad_out: bfloat16 [4096, 512], P('ep')
- expert_ids: int32 [4096, 2], P('ep')
- w_gate: bfloat16 [512, 8], replicated
- w_in: bfloat16 [8, 512, 2048], P('ep')
- w_out: bfloat16 [8, 2048, 512], P('ep')
Outputs:
- output 1: bfloat16 [4096, 512], P('ep')
- output 2: bfloat16 [4096, 512], P('ep')
- output 3: float32 [8, 512, 2048], P('ep')
- output 4: float32 [8, 2048, 512], P('ep')
- output 5: float32 [512, 8], replicated
All inputs are finite; a program needn't handle non-finite values.
Results may differ from a plain program's by a relative error of at most 0.00501279.
Values are sent between devices in bfloat16 or wider.
A program may use at most 1 GiB of HBM per device.

v0:
```python
import jax
import jax.numpy as jnp
from jax import lax
from jax.sharding import PartitionSpec as P


def route_slots(expert_ids, n_exp):
    flat_ids = expert_ids.reshape(-1)
    one_hot = (flat_ids[:, None] == jnp.arange(n_exp)[None, :]).astype(jnp.int32)
    rank_in = jnp.sum((jnp.cumsum(one_hot, axis=0) - one_hot) * one_hot, axis=1)
    return flat_ids, one_hot, rank_in


def slot_owner(dest_slot, n_slots):
    n_choice = dest_slot.shape[0]
    return jnp.full((n_slots,), n_choice, jnp.int32).at[dest_slot].set(jnp.arange(n_choice, dtype=jnp.int32), mode='drop')


def local_block(tokens, grad_out, expert_ids, w_gate, w_in, w_out):
    n_exp = w_gate.shape[1]
    tok_dev, d_model = tokens.shape
    cap_rows = tok_dev // 4
    n_choice = 2 * tok_dev
    n_slots = n_exp * cap_rows
    w_one = w_in[0]
    w_two = w_out[0]
    flat_ids, one_hot, rank_in = route_slots(expert_ids, n_exp)
    dest_slot = flat_ids * cap_rows + rank_in
    src_choice = slot_owner(dest_slot, n_slots)
    zero_row = jnp.zeros((1, d_model), jnp.bfloat16)
    x_table = jnp.concatenate([tokens, zero_row], axis=0)
    send_x = jnp.take(x_table, jnp.where(src_choice < n_choice, src_choice // 2, tok_dev), axis=0)
    recv_x = lax.all_to_all(send_x.reshape(n_exp, cap_rows, d_model), 'ep', 0, 0, tiled=True).reshape(n_slots, d_model)
    a_pre = jnp.dot(recv_x, w_one, preferred_element_type=jnp.float32)
    hidden, gelu_vjp = jax.vjp(jax.nn.gelu, a_pre)
    hid_b = hidden.astype(jnp.bfloat16)
    y_rows = jnp.dot(hid_b, w_two, preferred_element_type=jnp.float32).astype(jnp.bfloat16)
    y_back = lax.all_to_all(y_rows.reshape(n_exp, cap_rows, d_model), 'ep', 0, 0, tiled=True).reshape(n_slots, d_model)
    y_pair = jnp.take(y_back, dest_slot, axis=0).reshape(tok_dev, 2, d_model)
    logits = jnp.dot(tokens, w_gate, preferred_element_type=jnp.float32)
    choice_hot = one_hot.reshape(tok_dev, 2, n_exp) > 0
    sel_logit = jnp.sum(jnp.where(choice_hot, logits[:, None, :], 0.0), axis=-1)
    gate_val = jax.nn.softmax(sel_logit, axis=1)
    y_out = jnp.sum(gate_val[:, :, None] * y_pair.astype(jnp.float32), axis=1).astype(jnp.bfloat16)
    d_gate = jnp.einsum('tm,tkm->tk', grad_out, y_pair, preferred_element_type=jnp.float32)
    dy_flat = (gate_val[:, :, None] * grad_out[:, None, :].astype(jnp.float32)).astype(jnp.bfloat16).reshape(n_choice, d_model)
    send_dy = jnp.take(jnp.concatenate([dy_flat, zero_row], axis=0), src_choice, axis=0)
    recv_dy = lax.all_to_all(send_dy.reshape(n_exp, cap_rows, d_model), 'ep', 0, 0, tiled=True).reshape(n_slots, d_model)
    g_w_out = jnp.einsum('rh,rm->hm', hid_b, recv_dy, preferred_element_type=jnp.float32)
    d_hid = jnp.einsum('rm,hm->rh', recv_dy, w_two, preferred_element_type=jnp.float32)
    d_pre = gelu_vjp(d_hid)[0].astype(jnp.bfloat16)
    g_w_in = jnp.einsum('rm,rh->mh', recv_x, d_pre, preferred_element_type=jnp.float32)
    dx_rows = jnp.einsum('rh,mh->rm', d_pre, w_one, preferred_element_type=jnp.float32).astype(jnp.bfloat16)
    dx_back = lax.all_to_all(dx_rows.reshape(n_exp, cap_rows, d_model), 'ep', 0, 0, tiled=True).reshape(n_slots, d_model)
    dx_pair = jnp.take(dx_back, dest_slot, axis=0).reshape(tok_dev, 2, d_model)
    d_sel = gate_val * (d_gate - jnp.sum(gate_val * d_gate, axis=1, keepdims=True))
    d_logits = jnp.sum(jnp.where(choice_hot, d_sel[:, :, None], 0.0), axis=1).astype(jnp.bfloat16)
    grad_x = (jnp.sum(dx_pair.astype(jnp.float32), axis=1) + jnp.einsum('te,me->tm', d_logits, w_gate, preferred_element_type=jnp.float32)).astype(jnp.bfloat16)
    grad_w_gate = lax.psum(jnp.einsum('tm,te->me', tokens, d_logits, preferred_element_type=jnp.float32), 'ep')
    return y_out, grad_x, g_w_in[None], g_w_out[None], grad_w_gate


def solution(mesh):
    return jax.shard_map(local_block, mesh=mesh, in_specs=(P('ep'), P('ep'), P('ep'), P(), P('ep'), P('ep')), out_specs=(P('ep'), P('ep'), P('ep'), P('ep'), P()), check_vma=False)
```

profile of v0, /device:TPU:0, one launch (start us, length us, event | category | flops | bytes accessed | tf_op | source)
XLA Modules:
  0.0 176.8 jit_solution(13643506739122665493)
XLA Ops:
  5.9 4.3 %scatter_custom_fusion = s32[1024]{0:T(1024)S(1)} fusion(s32[1024]{0:T(1024)S(1)} %bitcast.90, s32[1024]{0:T(1024)S(1)} %iota.15, s32[]{:T(128)} %constant.46.clone.1), kind=kCustom, calls=%fused_computation.78 | custom fusion | bytes 4100 | tf_op jit(solution)/shard_map/scatter | solution.py:16
  11.3 5.1 %gather_fusion = bf16[1024,512]{1,0:T(8,128)(2,1)} fusion(bf16[513,512]{1,0:T(8,128)(2,1)S(1)} %concatenate.6, s32[1024]{0:T(1024)S(1)} %get-tuple-element.11), kind=kCustom, calls=%fused_computation.2 | custom fusion | bytes 2101248 | tf_op jit(solution)/shard_map/jit(_take)/gather | solution.py:32
  17.8 19.4 %all_to_all.20 = bf16[8,128,512]{2,1,0:T(8,128)(2,1)S(1)} all-to-all(bf16[8,128,512]{2,1,0:T(8,128)(2,1)S(1)} %broadcast_select_fusion.2), channel_id=1, replica_groups=mesh['ep'=8] {'ep'}, dimensions={0} | all-to-all | bytes 2097152 | tf_op jit(solution)/shard_map/all_to_all | solution.py:33
  38.3 3.9 %fusion.15 = f32[1024,2048]{1,0:T(8,128)S(1)} fusion(bf16[1024,512]{1,0:T(8,128)(2,1)S(1)} %bitcast.79, bf16[1,512,2048]{2,1,0:T(8,128)(2,1)} %param.12), kind=kOutput, calls=%fused_computation.23 | convolution fusion | flops 2147483648 | bytes 11534336 | tf_op jit(solution)/shard_map/dot_general | solution.py:34
  42.3 3.7 %fusion.20 = bf16[1024,512]{1,0:T(8,128)(2,1)} fusion(bf16[1,2048,512]{2,1,0:T(8,128)(2,1)S(1)} %copy-done, f32[1024,2048]{1,0:T(8,128)S(1)} %fusion.15), kind=kOutput, calls=%fused_computation.28 | convolution fusion | flops 2166882304 | bytes 11534336 | tf_op jit(solution)/shard_map/dot_general | solution.py:37
  46.0 2.4 %all-to-all-start.1 = ((bf16[8,128,512]{2,1,0:T(8,128)(2,1)}), bf16[8,128,512]{2,1,0:T(8,128)(2,1)S(1)}, u32[]{:S(2)}, u32[]{:S(2)}) async-start(bf16[8,128,512]{2,1,0:T(8,128)(2,1)} %bitcast.85), calls=%async_computation.1 | async-start | bytes 2097152 | tf_op jit(solution)/shard_map/all_to_all | solution.py:38
  48.5 2.9 %mul.110 = f32[512,2,512]{2,1,0:T(2,128)} broadcast(bf16[512,512]{1,0:T(8,128)(2,1)} %param.9), dimensions={0,2} | broadcast | bytes 2621440 | tf_op jit(solution)/shard_map/mul | solution.py:46
  51.4 3.6 %mul.111 = f32[1024,512]{1,0:T(8,128)} reshape(f32[512,2,512]{2,1,0:T(2,128)} %mul.110) | data formatting | bytes 4194304 | tf_op jit(solution)/shard_map/mul | solution.py:46
  56.4 7.3 %all-to-all-done.1 = bf16[8,128,512]{2,1,0:T(8,128)(2,1)S(1)} async-done(((bf16[8,128,512]{2,1,0:T(8,128)(2,1)}), bf16[8,128,512]{2,1,0:T(8,128)(2,1)S(1)}, u32[]{:S(2)}, u32[]{:S(2)}) %all-to-all-start.1) | async-done | bytes 1048608 | tf_op jit(solution)/shard_map/all_to_all | solution.py:38
  63.7 5.1 %gather_fusion.2 = bf16[1024,512]{1,0:T(8,128)(2,1)} fusion(bf16[1024,512]{1,0:T(8,128)(2,1)S(1)} %bitcast.77, s32[1024]{0:T(1024)S(1)} %broadcast_clamp_fusion), kind=kCustom, calls=%fused_computation.clone | custom fusion | bytes 2101248 | tf_op jit(solution)/shard_map/jit(_take)/gather | solution.py:39
  72.7 3.3 %fusion.24 = f32[512,1,2]{2,1,0:T(1,128)S(1)} fusion(bf16[512,2,512]{2,1,0:T(2,128)(2,1)S(1)} %reshape.172, bf16[512,512,1]{1,0,2:T(8,128)(2,1)} %bitcast.87), kind=kOutput, calls=%fused_computation.36 | convolution fusion | flops 1048576 | bytes 1576960 | tf_op jit(solution)/shard_map/tm,tkm->tk/dot_general | solution.py:45
  78.4 5.1 %gather_fusion.1 = bf16[1024,512]{1,0:T(8,128)(2,1)} fusion(bf16[1025,512]{1,0:T(8,128)(2,1)S(1)} %concatenate.7, s32[1024]{0:T(1024)S(1)} %get-tuple-element.10), kind=kCustom, calls=%fused_computation.3 | custom fusion | bytes 2101248 | tf_op jit(solution)/shard_map/jit(_take)/gather | solution.py:47
  89.4 30.6 %psum.7 = f32[512,8]{0,1:T(8,128)} all-reduce(f32[512,8]{0,1:T(8,128)S(1)} %convolution_bitcast_fusion.2), channel_id=1, replica_groups=mesh['ep'=8] {'ep'}, use_global_device_ids=true, to_apply=%region_11.13 | all-reduce | flops 4096 | bytes 32768 | tf_op jit(solution)/shard_map/psum | solution.py:59
  120.0 5.1 %multiply_reduce_fusion = bf16[512,512]{1,0:T(8,128)(2,1)} fusion(bf16[512,2,512]{2,1,0:T(2,128)(2,1)} %copy-done.3, f32[512,2]{1,0:T(8,128)S(1)} %copy.18), kind=kLoop, calls=%fused_computation.26 | loop fusion | flops 1310720 | bytes 1576960 | tf_op jit(solution)/shard_map/reduce_sum | solution.py:44
  125.0 9.2 %fusion.6 = bf16[1024,2048]{1,0:T(8,128)(2,1)S(1)} fusion(f32[1024,2048]{1,0:T(8,128)} %copy-done.8, bf16[1024,512]{1,0:T(8,128)(2,1)S(1)} %bitcast.83, bf16[1,2048,512]{2,1,0:T(8,128)(2,1)S(1)} %copy-done), kind=kOutput, calls=%fused_computation.13 | convolution fusion | flops 2189426688 | bytes 15728640 | tf_op jit(solution)/shard_map/rm,hm->rh/dot_general | solution.py:50
  134.2 3.3 %fusion.17 = bf16[1024,512]{1,0:T(8,128)(2,1)} fusion(bf16[1024,2048]{1,0:T(8,128)(2,1)S(1)} %fusion.6, bf16[1,512,2048]{2,1,0:T(8,128)(2,1)S(1)} %copy-done.7), kind=kOutput, calls=%fused_computation.27 | convolution fusion | flops 2148007936 | bytes 7340032 | tf_op jit(solution)/shard_map/rh,mh->rm/dot_general | solution.py:53
  137.6 4.5 %convolution_bitcast_fusion.1 = f32[1,512,2048]{2,1,0:T(8,128)} fusion(bf16[1024,512]{1,0:T(8,128)(2,1)S(1)} %bitcast.80, bf16[1024,2048]{1,0:T(8,128)(2,1)S(1)} %fusion.6), kind=kOutput, calls=%fused_computation.16 | convolution fusion | flops 2147483648 | bytes 9437184 | tf_op jit(solution)/shard_map/rm,rh->mh/dot_general | solution.py:52
  142.1 2.9 %all-to-all-start.3 = ((bf16[8,128,512]{2,1,0:T(8,128)(2,1)}), bf16[8,128,512]{2,1,0:T(8,128)(2,1)S(1)}, u32[]{:S(2)}, u32[]{:S(2)}) async-start(bf16[8,128,512]{2,1,0:T(8,128)(2,1)} %bitcast.86), calls=%async_computation.3 | async-start | bytes 2097152 | tf_op jit(solution)/shard_map/all_to_all | solution.py:54
  144.9 9.4 %convolution_bitcast_fusion = f32[1,2048,512]{2,1,0:T(8,128)} fusion(bf16[1024,512]{1,0:T(8,128)(2,1)} %bitcast.84, f32[1024,2048]{1,0:T(8,128)} %copy-done.8), kind=kOutput, calls=%fused_computation.15 | convolution fusion | flops 2166358016 | bytes 13631488 | tf_op jit(solution)/shard_map/rh,rm->hm/dot_general | solution.py:49
  154.3 6.0 %all-to-all-done.3 = bf16[8,128,512]{2,1,0:T(8,128)(2,1)S(1)} async-done(((bf16[8,128,512]{2,1,0:T(8,128)(2,1)}), bf16[8,128,512]{2,1,0:T(8,128)(2,1)S(1)}, u32[]{:S(2)}, u32[]{:S(2)}) %all-to-all-start.3) | async-done | bytes 1048608 | tf_op jit(solution)/shard_map/all_to_all | solution.py:54
  160.3 5.1 %gather_fusion.3 = bf16[1024,512]{1,0:T(8,128)(2,1)} fusion(bf16[1024,512]{1,0:T(8,128)(2,1)S(1)} %bitcast.78, s32[1024]{0:T(1024)S(1)} %broadcast_clamp_fusion), kind=kCustom, calls=%fused_computation.1.clone | custom fusion | bytes 2101248 | tf_op jit(solution)/shard_map/jit(_take)/gather | solution.py:55
  165.3 2.8 %select_convert_fusion = f32[1024,512]{1,0:T(8,128)} fusion(bf16[1024,512]{1,0:T(8,128)(2,1)} %gather_fusion.3, pred[1024]{0:T(1024)(128)(4,1)S(1)} %compare_and_fusion), kind=kLoop, calls=%fused_computation.32 | loop fusion | flops 1048576 | bytes 3146752 | tf_op jit(solution)/shard_map/convert_element_type | solution.py:58
  168.1 3.5 %reshape.176 = f32[512,2,512]{2,1,0:T(2,128)} reshape(f32[1024,512]{1,0:T(8,128)} %select_convert_fusion) | data formatting | bytes 4194304 | tf_op jit(solution)/shard_map/convert_element_type | solution.py:58
  171.6 4.1 %reduce_sum.70 = f32[512,512]{1,0:T(8,128)S(1)} reduce(f32[512,2,512]{2,1,0:T(2,128)} %reshape.176, f32[]{:T(128)} %constant.38.clone.1), dimensions={1}, to_apply=%region_8.10 | reduce | flops 262144 | bytes 3145732 | tf_op jit(solution)/shard_map/reduce_sum | solution.py:58
  (57 shorter events, 23.5 us)
Async XLA Ops:
  0.6 41.6 %copy-start = (bf16[1,2048,512]{2,1,0:T(8,128)(2,1)S(1)}, bf16[1,2048,512]{2,1,0:T(8,128)(2,1)}, u32[]{:S(2)}) copy-start(bf16[1,2048,512]{2,1,0:T(8,128)(2,1)} %param.13) | copy-start | bytes 6291460
  37.3 1.1 copy-start.1
  42.3 3.7 %copy-start.8 = (f32[1024,2048]{1,0:T(8,128)}, f32[1024,2048]{1,0:T(8,128)S(1)}, u32[]{:S(2)}) copy-start(f32[1024,2048]{1,0:T(8,128)S(1)} %fusion.15) | copy-start | bytes 25165828
  46.0 9.0 %copy-start.6 = (bf16[512,8]{0,1:T(8,128)(2,1)S(1)}, bf16[512,8]{0,1:T(8,128)(2,1)}, u32[]{:S(2)}) copy-start(bf16[512,8]{0,1:T(8,128)(2,1)} %param.11) | copy-start | bytes 24580
  46.0 10.3 %copy-start.5 = (s32[512,2]{0,1:T(2,128)S(1)}, s32[512,2]{0,1:T(2,128)}, u32[]{:S(2)}) copy-start(s32[512,2]{0,1:T(2,128)} %param.10) | copy-start | bytes 12292
  46.0 17.7 %all-to-all-start.1 = ((bf16[8,128,512]{2,1,0:T(8,128)(2,1)}), bf16[8,128,512]{2,1,0:T(8,128)(2,1)S(1)}, u32[]{:S(2)}, u32[]{:S(2)}) async-start(bf16[8,128,512]{2,1,0:T(8,128)(2,1)} %bitcast.85), calls=%async_computation.1 | async-start | bytes 2097152 | tf_op jit(solution)/shard_map/all_to_all | solution.py:38
  72.7 3.8 %copy-start.3 = (bf16[512,2,512]{2,1,0:T(2,128)(2,1)}, bf16[512,2,512]{2,1,0:T(2,128)(2,1)S(1)}, u32[]{:S(2)}) copy-start(bf16[512,2,512]{2,1,0:T(2,128)(2,1)S(1)} %reshape.172) | copy-start | bytes 3145732
  85.8 39.2 %all-to-all-start.2 = ((bf16[8,128,512]{2,1,0:T(8,128)(2,1)}), bf16[8,128,512]{2,1,0:T(8,128)(2,1)S(1)}, u32[]{:S(2)}, u32[]{:S(2)}) async-start(bf16[8,128,512]{2,1,0:T(8,128)(2,1)} %broadcast_select_fusion.1), calls=%async_computation.2 | async-start | bytes 2097152 | tf_op jit(solution)/shard_map/all_to_all | solution.py:48
  125.0 9.2 %copy-start.4 = (bf16[8,128,512]{2,1,0:T(8,128)(2,1)}, bf16[8,128,512]{2,1,0:T(8,128)(2,1)S(1)}, u32[]{:S(2)}) copy-start(bf16[8,128,512]{2,1,0:T(8,128)(2,1)S(1)} %all-to-all-done.2) | copy-start | bytes 3145732
  125.0 9.2 %copy-start.7 = (bf16[1,512,2048]{2,1,0:T(8,128)(2,1)S(1)}, bf16[1,512,2048]{2,1,0:T(8,128)(2,1)}, u32[]{:S(2)}) copy-start(bf16[1,512,2048]{2,1,0:T(8,128)(2,1)} %param.12) | copy-start | bytes 6291460
  134.2 3.4 %copy-start.2 = (bf16[8,128,512]{2,1,0:T(8,128)(2,1)S(1)}, bf16[8,128,512]{2,1,0:T(8,128)(2,1)}, u32[]{:S(2)}) copy-start(bf16[8,128,512]{2,1,0:T(8,128)(2,1)} %copy-done.1) | copy-start | bytes 3145732
  142.1 18.2 %all-to-all-start.3 = ((bf16[8,128,512]{2,1,0:T(8,128)(2,1)}), bf16[8,128,512]{2,1,0:T(8,128)(2,1)S(1)}, u32[]{:S(2)}, u32[]{:S(2)}) async-start(bf16[8,128,512]{2,1,0:T(8,128)(2,1)} %bitcast.86), calls=%async_computation.3 | async-start | bytes 2097152 | tf_op jit(solution)/shard_map/all_to_all | solution.py:54
where the time goes:
time: 178 us; the launch traced here: 177 us
  blocking collectives  50 us (28%)
  matrix products  40.9 us (23%)
  local copies, waits for them, and re-layouts  40.6 us (23%)
  other arithmetic  23.5 us (13%)
  waiting for transfers between devices  13.3 us (7%)
  starting transfers between devices  7.57 us (4%)
    psum x1, blocking collectives, local_block(): lax.psum(jnp.einsum('tm,te->me', tokens, d_logits, preferred_element_type...  30.6 us
    all_to_all x1, blocking collectives, local_block(): lax.all_to_all(send_x.reshape(n_exp, cap_rows, d_model), 'ep', 0, 0, tile...  19.4 us
    dot_general x1, matrix products, local_block(): jnp.einsum('rh,rm->hm', hid_b, recv_dy, preferred_element_type=jnp.float32)  9.36 us
    dot_general x1, matrix products, local_block(): jnp.einsum('rm,hm->rh', recv_dy, w_two, preferred_element_type=jnp.float32)  9.16 us
    all_to_all x1, waiting for transfers between devices, local_block(): lax.all_to_all(y_rows.reshape(n_exp, cap_rows, d_model), 'ep', 0, 0, tile...  7.33 us
    mul x2, local copies, waits for them, and re-layouts, local_block(): gate_val[:, :, None] * grad_out[:, None, :].astype(jnp.float32)  6.55 us
    all_to_all x1, waiting for transfers between devices, local_block(): lax.all_to_all(dx_rows.reshape(n_exp, cap_rows, d_model), 'ep', 0, 0, til...  5.99 us
    gather x1, local copies, waits for them, and re-layouts, local_block(): jnp.take(x_table, jnp.where(src_choice < n_choice, src_choice // 2, tok_d...  5.08 us
  transfers between devices with their start and end apart: 3, of which 2 were waited for; matrix products, arithmetic and copies ran while one was open for 13% of the time, Pallas kernels for 0%

commit v1 on v0

v1 whole, which is shorter than its diff:
```python
import functools

import jax
import jax.numpy as jnp
from jax import lax
from jax.experimental import pallas as pl
from jax.experimental.pallas import tpu as pltpu
from jax.sharding import PartitionSpec as P

N_DEV = 8
ROWS = 128
MESH = pl.DeviceIdType.MESH
F32 = jnp.float32
BF16 = jnp.bfloat16
SQRT_2_PI = 0.7978845608028654
CUBIC = 0.044715


def dot_nn(a, b):
    return lax.dot_general(a, b, (((1,), (0,)), ((), ())), preferred_element_type=F32)


def dot_nt(a, b):
    return lax.dot_general(a, b, (((1,), (1,)), ((), ())), preferred_element_type=F32)


def dot_tn(a, b):
    return lax.dot_general(a, b, (((0,), (0,)), ((), ())), preferred_element_type=F32)


def moe_kernel(ids_ref, wgt_ref, x_hbm, dout_hbm, win_hbm, wout_hbm,
               out_ref, gx_ref, gwin_ref, gwout_ref, gwg_ref,
               x_v, dout_v, win_v, wout_v, rank_v, p_v, q0_v, q1_v, dyflat_v, gate_v, cols_v,
               sx, rx, sdy, rdy, sy, ry, sdx, rdx, h_v, gp_v, da_v, xt_v, wg_part, wg_all,
               load_sem, send_sem, recv_sem, wg_send, wg_recv):
    tok = x_v.shape[0]
    d_hid = win_v.shape[1]
    me = lax.axis_index('ep')
    core, col, row = me % 2, (me // 2) % 2, me // 4

    def peer(d):
        return 4 * ((row + d // 4) % 2) + 2 * ((col + (d // 2) % 2) % 2) + (core + d % 2) % 2

    def remote(phase, src, dst, d):
        return pltpu.make_async_remote_copy(
            src_ref=src.at[pl.ds(d * ROWS, ROWS)], dst_ref=dst.at[pl.ds(d * ROWS, ROWS)], send_sem=send_sem.at[phase, d], recv_sem=recv_sem.at[phase, d],
            device_id=(peer(d),), device_id_type=MESH)

    barrier = pltpu.get_barrier_semaphore()
    for d in range(1, N_DEV):
        pl.semaphore_signal(barrier, inc=1, device_id=(peer(d),), device_id_type=MESH)
    loads = [pltpu.make_async_copy(src, dst, load_sem.at[i]) for i, (src, dst) in enumerate(
        ((x_hbm, x_v), (dout_hbm, dout_v), (win_hbm, win_v), (wout_hbm, wout_v)))]
    for ld in loads:
        ld.start()

    rel = lax.broadcasted_iota(jnp.int32, (16, tok), 0) ^ me
    ids0 = ids_ref[0:1, :]
    ids1 = ids_ref[1:2, :]
    hit0 = rel == ids0
    hit1 = rel == ids1
    hot = jnp.where(hit0 | hit1, 1.0, 0.0).astype(BF16)
    before = jnp.where(lax.broadcasted_iota(jnp.int32, (tok, tok), 0) < lax.broadcasted_iota(jnp.int32, (tok, tok), 1), 1.0, 0.0).astype(BF16)
    rank = dot_nn(hot, before)
    rank0 = jnp.where(hit0, rank, -1.0)
    rank1 = jnp.where(hit1, rank, -1.0)
    rank_v[0:16, :] = rank0
    rank_v[16:32, :] = rank1
    slot = lax.broadcasted_iota(jnp.int32, (ROWS, tok), 0).astype(F32)

    loads[0].wait()
    pl.semaphore_wait(barrier, N_DEV - 1)
    for d in (2, 4, 3, 5, 6, 7, 1, 0):
        pick0 = jnp.where(rank_v[d:d + 1, :] == slot, 1.0, 0.0)
        pick1 = jnp.where(rank_v[16 + d:17 + d, :] == slot, 1.0, 0.0)
        block = dot_nn((pick0 + pick1).astype(BF16), x_v[...]).astype(BF16)
        if d == 0:
            rx[0:ROWS] = block
        else:
            sx[d * ROWS:(d + 1) * ROWS] = block
            remote(0, sx, rx, d).start()
        p_v[d, :, 0:tok] = pick0.astype(BF16)
        p_v[d, :, tok:2 * tok] = pick1.astype(BF16)

    stack = jnp.concatenate([rank0, rank1, jnp.broadcast_to(ids0.astype(F32), (16, tok)),
                             jnp.broadcast_to(ids1.astype(F32), (16, tok)), jnp.zeros((64, tok), F32)], axis=0)
    cols_v[...] = stack.T
    logits = dot_nt(x_v[...], wgt_ref[...])
    lane8 = lax.broadcasted_iota(jnp.int32, (tok, N_DEV), 1).astype(F32)
    sel0 = jnp.sum(jnp.where(lane8 == cols_v[:, 32:33], logits, 0.0), axis=1, keepdims=True)
    sel1 = jnp.sum(jnp.where(lane8 == cols_v[:, 48:49], logits, 0.0), axis=1, keepdims=True)
    top = jnp.maximum(sel0, sel1)
    e0 = jnp.exp(sel0 - top)
    e1 = jnp.exp(sel1 - top)
    gate_v[0] = e0 / (e0 + e1)
    gate_v[1] = e1 / (e0 + e1)
    loads[1].wait()
    dout_f = dout_v[...].astype(F32)
    dyflat_v[0:tok, :] = (gate_v[0] * dout_f).astype(BF16)
    dyflat_v[tok:2 * tok, :] = (gate_v[1] * dout_f).astype(BF16)
    for d in (2, 4, 3, 5, 6, 7, 1, 0):
        block = dot_nn(p_v[d], dyflat_v[...]).astype(BF16)
        if d == 0:
            rdy[0:ROWS] = block
        else:
            sdy[d * ROWS:(d + 1) * ROWS] = block
            remote(1, sdy, rdy, d).start()

    hid = 512
    loads[2].wait()
    loads[3].wait()
    for c in range(4):
        for d in (2 * c, 2 * c + 1):
            if d:
                remote(0, sx, rx, d).wait_recv()
        rows = slice(2 * ROWS * c, 2 * ROWS * (c + 1))
        x_c = rx[rows]

        def fwd_tile(j, carry):
            cols = pl.ds(pl.multiple_of(j * hid, hid), hid)
            a = dot_nn(x_c, win_v[:, cols])
            sq = a * a
            t = jnp.tanh(SQRT_2_PI * (a + CUBIC * (a * sq)))
            cdf = 0.5 * (1.0 + t)
            h_v[rows, cols] = (a * cdf).astype(BF16)
            gp_v[rows, cols] = cdf + (0.5 * a) * (1.0 - t * t) * (SQRT_2_PI * (1.0 + (3.0 * CUBIC) * sq))
            return carry

        lax.fori_loop(0, d_hid // hid, fwd_tile, 0)
        y_c = dot_nn(h_v[rows, :], wout_v[...]).astype(BF16)
        for i, d in enumerate((2 * c, 2 * c + 1)):
            block = y_c[i * ROWS:(i + 1) * ROWS]
            if d == 0:
                ry[0:ROWS] = block
            else:
                sy[d * ROWS:(d + 1) * ROWS] = block
                remote(2, sy, ry, d).start()

    slot_l = lax.broadcasted_iota(jnp.int32, (tok, ROWS), 1).astype(F32)
    for d in range(N_DEV):
        q0_v[:, d * ROWS:(d + 1) * ROWS] = jnp.where(cols_v[:, d:d + 1] == slot_l, 1.0, 0.0).astype(BF16)
        q1_v[:, d * ROWS:(d + 1) * ROWS] = jnp.where(cols_v[:, 16 + d:17 + d] == slot_l, 1.0, 0.0).astype(BF16)

    def bwd_chunk(c):
        for d in (2 * c, 2 * c + 1):
            if d:
                remote(1, sdy, rdy, d).wait_recv()
        rows = slice(2 * ROWS * c, 2 * ROWS * (c + 1))
        dy_c = rdy[rows]

        def bwd_tile(j, carry):
            cols = pl.ds(pl.multiple_of(j * hid, hid), hid)
            dh = dot_nt(dy_c, wout_v[cols, :])
            da_v[rows, cols] = (dh * gp_v[rows, cols]).astype(BF16)
            return carry

        lax.fori_loop(0, d_hid // hid, bwd_tile, 0)
        dx_c = dot_nt(da_v[rows, :], win_v[...]).astype(BF16)
        for i, d in enumerate((2 * c, 2 * c + 1)):
            block = dx_c[i * ROWS:(i + 1) * ROWS]
            if d == 0:
                rdx[0:ROWS] = block
            else:
                sdx[d * ROWS:(d + 1) * ROWS] = block
                if c < 3:
                    remote(3, sdx, rdx, d).start()

    for c in range(4):
        bwd_chunk(c)

    xt_v[...] = rx[...].T
    wt = 256

    def grad_tile(j, carry):
        cols = pl.ds(pl.multiple_of(j * wt, wt), wt)
        gwout_ref[cols, :] = dot_tn(h_v[:, cols], rdy[...])
        gwin_ref[:, cols] = dot_nn(xt_v[...], da_v[:, cols])
        return carry

    lax.fori_loop(0, d_hid // wt, grad_tile, 0)

    for d in range(1, N_DEV):
        remote(2, sy, ry, d).wait_recv()
    y0 = dot_nn(q0_v[...], ry[...])
    y1 = dot_nn(q1_v[...], ry[...])
    g0 = gate_v[0]
    g1 = gate_v[1]
    dout_f = dout_v[...].astype(F32)
    out_ref[...] = (g0 * y0 + g1 * y1).astype(BF16)
    dg0 = jnp.sum(dout_f * y0, axis=1, keepdims=True)
    dg1 = jnp.sum(dout_f * y1, axis=1, keepdims=True)
    mean = g0 * dg0 + g1 * dg1
    d_log = (jnp.where(lane8 == cols_v[:, 32:33], g0 * (dg0 - mean), 0.0)
             + jnp.where(lane8 == cols_v[:, 48:49], g1 * (dg1 - mean), 0.0)).astype(BF16)
    wg_part[...] = dot_tn(d_log, x_v[...])
    wg_all[me] = wg_part[...]

    def wg_copy(d):
        return pltpu.make_async_remote_copy(
            src_ref=wg_part, dst_ref=wg_all.at[me], send_sem=wg_send.at[d], recv_sem=wg_recv.at[d],
            device_id=(peer(d),), device_id_type=MESH)

    for d in range(1, N_DEV):
        wg_copy(d).start()
    for d in (6, 7):
        remote(3, sdx, rdx, d).start()
    acc = dot_nn(d_log, wgt_ref[...])

    for c in range(4):
        for d in (2 * c, 2 * c + 1):
            if d:
                remote(3, sdx, rdx, d).wait_recv()
        span = slice(2 * ROWS * c, 2 * ROWS * (c + 1))
        acc = acc + dot_nn(q0_v[:, span] + q1_v[:, span], rdx[span])
    gx_ref[...] = acc.astype(BF16)
    for d in range(1, N_DEV):
        wg_copy(d).wait_recv()
    total = wg_all[0]
    for s in range(1, N_DEV):
        total = total + wg_all[s]
    gwg_ref[...] = total
    for d in range(1, N_DEV):
        remote(0, sx, rx, d).wait_send()
        remote(1, sdy, rdy, d).wait_send()
        remote(2, sy, ry, d).wait_send()
        remote(3, sdx, rdx, d).wait_send()
        wg_copy(d).wait_send()


def local_block(tokens, grad_out, expert_ids, w_gate, w_in, w_out):
    tok, d_model = tokens.shape
    n_exp = w_gate.shape[1]
    d_hid = w_in.shape[2]
    slots = n_exp * ROWS
    vmem = pl.BlockSpec(memory_space=pltpu.VMEM)
    hbm = pl.BlockSpec(memory_space=pl.ANY)
    blocks = pltpu.VMEM((slots, d_model), BF16)
    out, gx, gwin, gwout, gwg = pl.pallas_call(
        moe_kernel,
        out_shape=(jax.ShapeDtypeStruct((tok, d_model), BF16), jax.ShapeDtypeStruct((tok, d_model), BF16),
                   jax.ShapeDtypeStruct((d_model, d_hid), F32), jax.ShapeDtypeStruct((d_hid, d_model), F32),
                   jax.ShapeDtypeStruct((n_exp, d_model), F32)),
        in_specs=[vmem, vmem, hbm, hbm, hbm, hbm],
        out_specs=(vmem,) * 5,
        scratch_shapes=[
            pltpu.VMEM((tok, d_model), BF16), pltpu.VMEM((tok, d_model), BF16),
            pltpu.VMEM((d_model, d_hid), BF16), pltpu.VMEM((d_hid, d_model), BF16),
            pltpu.VMEM((32, tok), F32), pltpu.VMEM((n_exp, ROWS, 2 * tok), BF16),
            pltpu.VMEM((tok, slots), BF16), pltpu.VMEM((tok, slots), BF16),
            pltpu.VMEM((2 * tok, d_model), BF16), pltpu.VMEM((2, tok, 1), F32), pltpu.VMEM((tok, 128), F32),
            blocks, blocks, blocks, blocks, blocks, blocks, blocks, blocks,
            pltpu.VMEM((slots, d_hid), BF16), pltpu.VMEM((slots, d_hid), F32), pltpu.VMEM((slots, d_hid), BF16),
            pltpu.VMEM((d_model, slots), BF16), pltpu.VMEM((n_exp, d_model), F32), pltpu.VMEM((n_exp, n_exp, d_model), F32),
            pltpu.SemaphoreType.DMA((4,)), pltpu.SemaphoreType.DMA((4, n_exp)), pltpu.SemaphoreType.DMA((4, n_exp)),
            pltpu.SemaphoreType.DMA((n_exp,)), pltpu.SemaphoreType.DMA((n_exp,)),
        ],
        compiler_params=pltpu.CompilerParams(collective_id=0, has_side_effects=True, vmem_limit_bytes=47 * 1024 * 1024),
        name='moe_step',
    )(expert_ids.T, w_gate.T, tokens, grad_out, w_in[0], w_out[0])
    return out, gx, gwin[None], gwout[None], gwg.T


def solution(mesh):
    return jax.shard_map(local_block, mesh=mesh, in_specs=(P('ep'), P('ep'), P('ep'), P(), P('ep'), P('ep')), out_specs=(P('ep'), P('ep'), P('ep'), P('ep'), P()), check_vma=False)
```

time: 178 us -> 73.5 us (0.41)
  Pallas kernels: 0 us -> 56.8 us
  blocking collectives: 50 us -> 0 us
  matrix products: 40.9 us -> 0 us
  local copies, waits for them, and re-layouts: 40.6 us -> 15.7 us
  other arithmetic: 23.5 us -> 0 us
  waiting for transfers between devices: 13.3 us -> 0 us
  starting transfers between devices: 7.57 us -> 0 us
    pallas_call x0 -> x1, Pallas kernels: none -> 56.8 us  [local_block(): pl.pallas_call(moe_kernel, out_shape=(jax.ShapeDtypeStruct((tok, d_model)...]
    dot_general x10 -> x0, matrix products: 40.9 us -> none  [the longest x1 9.36 us: local_block(): jnp.einsum('rh,rm->hm', hid_b, recv_dy, preferred_element_type=jnp.float32)]
    psum x1 -> x0, blocking collectives: 30.6 us -> none  [local_block(): lax.psum(jnp.einsum('tm,te->me', tokens, d_logits, preferred_element_type...]
    gather x4 -> x0, local copies, waits for them, and re-layouts: 20.3 us -> none  [the longest x1 5.08 us: local_block(): jnp.take(x_table, jnp.where(src_choice < n_choice, src_choice // 2, tok_d...]
    all_to_all x1 -> x0, blocking collectives: 19.4 us -> none  [local_block(): lax.all_to_all(send_x.reshape(n_exp, cap_rows, d_model), 'ep', 0, 0, tile...]
    unnamed x19, local copies, waits for them, and re-layouts: 1.93 us -> 15.7 us
    all_to_all x3 -> x0, waiting for transfers between devices: 13.3 us -> none  [the longest x1 7.33 us: local_block(): lax.all_to_all(y_rows.reshape(n_exp, cap_rows, d_model), 'ep', 0, 0, tile...]
    reduce_sum x7 -> x0, other arithmetic: 9.29 us -> none  [the longest x1 5.07 us: local_block(): jnp.sum(gate_val[:, :, None] * y_pair.astype(jnp.float32), axis=1)]
  transfers between devices with their start and end apart: 3 -> 0, of which waited for: 2 -> 0; matrix products, arithmetic and copies ran while one was open for 13% -> 0% of each run, Pallas kernels for 0% -> 0%
where the time goes in v1:
time: 73.5 us; the launch traced here: 73.2 us
  Pallas kernels  56.8 us (77%)
  local copies, waits for them, and re-layouts  15.7 us (21%)
    pallas_call x1, Pallas kernels, local_block(): pl.pallas_call(moe_kernel, out_shape=(jax.ShapeDtypeStruct((tok, d_model)...  56.8 us
    unnamed x19, local copies, waits for them, and re-layouts  15.7 us

profile of v1, /device:TPU:0, one launch (start us, length us, event | category | flops | bytes accessed | tf_op | source)
XLA Modules:
  0.0 73.2 jit_solution(16438231910975903733)
XLA Ops:
  0.6 0.0 copy-start
  0.6 1.6 %copy-done = bf16[1,512,2048]{2,1,0:T(8,128)(2,1)S(1)} copy-done((bf16[1,512,2048]{2,1,0:T(8,128)(2,1)S(1)}, bf16[1,512,2048]{2,1,0:T(8,128)(2,1)}, u32[]{:S(2)}) %copy-start) | copy-done | bytes 2097176
  2.2 0.0 copy-start.1
  2.2 1.6 %copy-done.1 = bf16[1,2048,512]{2,1,0:T(8,128)(2,1)S(1)} copy-done((bf16[1,2048,512]{2,1,0:T(8,128)(2,1)S(1)}, bf16[1,2048,512]{2,1,0:T(8,128)(2,1)}, u32[]{:S(2)}) %copy-start.1) | copy-done | bytes 2097176
  3.8 0.0 copy-start.2
  3.8 1.0 %copy-done.2 = bf16[512,512]{1,0:T(8,128)(2,1)S(1)} copy-done((bf16[512,512]{1,0:T(8,128)(2,1)S(1)}, bf16[512,512]{1,0:T(8,128)(2,1)}, u32[]{:S(2)}) %copy-start.2) | copy-done | bytes 524312
  4.9 0.0 copy-start.3
  4.9 1.0 %copy-done.3 = bf16[512,512]{1,0:T(8,128)(2,1)S(1)} copy-done((bf16[512,512]{1,0:T(8,128)(2,1)S(1)}, bf16[512,512]{1,0:T(8,128)(2,1)}, u32[]{:S(2)}) %copy-start.3) | copy-done | bytes 524312
  5.9 0.0 copy-start.4
  5.9 0.7 copy-done.4
  6.6 0.0 copy-start.5
  6.6 0.7 copy-done.5
  7.3 56.8 %moe_step.1 = (bf16[512,512]{1,0:T(8,128)(2,1)S(1)}, bf16[512,512]{1,0:T(8,128)(2,1)S(1)}, f32[512,2048]{1,0:T(8,128)}, f32[2048,512]{1,0:T(8,128)}, f32[8,512]{1,0:T(8,128)S(1)}) custom-call(s32[2,512]{1,0:T(2,128)S(1)} %bitcast.11, bf16[8,512]{1,0:T(8,128)(2,1)S(1)} %bitcast.10, bf16[512,512]{1,0:T(8,128)(2,1)S(1)} %copy-done.2, ...), custom_call_target="tpu_custom_call" | custom-call | tf_op jit(solution)/shard_map/moe_step/pallas_call | solution.py:238
  64.1 0.8 %copy.16 = bf16[512,512]{1,0:T(8,128)(2,1)} copy(bf16[512,512]{1,0:T(8,128)(2,1)S(1)} %get-tuple-element.20) | data formatting | bytes 1048576
  64.9 0.8 %copy.17 = bf16[512,512]{1,0:T(8,128)(2,1)} copy(bf16[512,512]{1,0:T(8,128)(2,1)S(1)} %get-tuple-element.21) | data formatting | bytes 1048576
  65.7 0.0 copy-start.6
  65.7 4.8 %copy.18 = f32[1,512,2048]{2,1,0:T(8,128)} copy(f32[1,512,2048]{2,1,0:T(8,128)} %bitcast.13) | data formatting | bytes 8388608
  70.5 0.0 copy-done.6
  70.5 2.0 %copy.19 = f32[1,2048,512]{2,1,0:T(8,128)} copy(f32[1,2048,512]{2,1,0:T(8,128)S(1)} %bitcast.12) | data formatting | bytes 8388608
  72.6 0.6 copy.20
Async XLA Ops:
  0.6 1.6 %copy-start = (bf16[1,512,2048]{2,1,0:T(8,128)(2,1)S(1)}, bf16[1,512,2048]{2,1,0:T(8,128)(2,1)}, u32[]{:S(2)}) copy-start(bf16[1,512,2048]{2,1,0:T(8,128)(2,1)} %param.10) | copy-start | bytes 6291460
  2.2 1.6 %copy-start.1 = (bf16[1,2048,512]{2,1,0:T(8,128)(2,1)S(1)}, bf16[1,2048,512]{2,1,0:T(8,128)(2,1)}, u32[]{:S(2)}) copy-start(bf16[1,2048,512]{2,1,0:T(8,128)(2,1)} %param.11) | copy-start | bytes 6291460
  3.8 1.0 %copy-start.2 = (bf16[512,512]{1,0:T(8,128)(2,1)S(1)}, bf16[512,512]{1,0:T(8,128)(2,1)}, u32[]{:S(2)}) copy-start(bf16[512,512]{1,0:T(8,128)(2,1)} %x_hbm.1) | copy-start | bytes 1572868
  4.9 1.0 %copy-start.3 = (bf16[512,512]{1,0:T(8,128)(2,1)S(1)}, bf16[512,512]{1,0:T(8,128)(2,1)}, u32[]{:S(2)}) copy-start(bf16[512,512]{1,0:T(8,128)(2,1)} %dout_hbm.1) | copy-start | bytes 1572868
  5.9 0.7 copy-start.4
  6.6 0.7 copy-start.5
  65.7 4.9 %copy-start.6 = (f32[2048,512]{1,0:T(8,128)S(1)}, f32[2048,512]{1,0:T(8,128)}, u32[]{:S(2)}) copy-start(f32[2048,512]{1,0:T(8,128)} %get-tuple-element.13) | copy-start | bytes 12582916

commit v2 on v1

--- a/solution.py
+++ b/solution.py
@@ -28,10 +28,10 @@
     return lax.dot_general(a, b, (((0,), (0,)), ((), ())), preferred_element_type=F32)
 
 
-def moe_kernel(ids_ref, wgt_ref, x_hbm, dout_hbm, win_hbm, wout_hbm,
-               out_ref, gx_ref, gwin_ref, gwout_ref, gwg_ref,
-               x_v, dout_v, win_v, wout_v, rank_v, p_v, q0_v, q1_v, dyflat_v, gate_v, cols_v,
-               sx, rx, sdy, rdy, sy, ry, sdx, rdx, h_v, gp_v, da_v, xt_v, wg_part, wg_all,
+def moe_kernel(ids_hbm, wgt_hbm, x_hbm, dout_hbm, win_hbm, wout_hbm,
+               out_ref, gwin_ref, gwout_ref, gwg_ref, acc_ref, qlast_ref, rdx,
+               ids_ref, wgt_ref, x_v, dout_v, win_v, wout_v, rank_v, p_v, q0_v, q1_v, dyflat_v, gate_v, cols_v,
+               sx, rx, sdy, rdy, sy, ry, sdx, h_v, gp_v, da_v, xt_v, wg_part, wg_all,
                load_sem, send_sem, recv_sem, wg_send, wg_recv):
     tok = x_v.shape[0]
     d_hid = win_v.shape[1]
@@ -50,11 +50,12 @@
     for d in range(1, N_DEV):
         pl.semaphore_signal(barrier, inc=1, device_id=(peer(d),), device_id_type=MESH)
     loads = [pltpu.make_async_copy(src, dst, load_sem.at[i]) for i, (src, dst) in enumerate(
-        ((x_hbm, x_v), (dout_hbm, dout_v), (win_hbm, win_v), (wout_hbm, wout_v)))]
+        ((ids_hbm, ids_ref), (x_hbm, x_v), (wgt_hbm, wgt_ref), (dout_hbm, dout_v), (win_hbm, win_v), (wout_hbm, wout_v)))]
     for ld in loads:
         ld.start()
 
     rel = lax.broadcasted_iota(jnp.int32, (16, tok), 0) ^ me
+    loads[0].wait()
     ids0 = ids_ref[0:1, :]
     ids1 = ids_ref[1:2, :]
     hit0 = rel == ids0
@@ -68,7 +69,7 @@
     rank_v[16:32, :] = rank1
     slot = lax.broadcasted_iota(jnp.int32, (ROWS, tok), 0).astype(F32)
 
-    loads[0].wait()
+    loads[1].wait()
     pl.semaphore_wait(barrier, N_DEV - 1)
     for d in (2, 4, 3, 5, 6, 7, 1, 0):
         pick0 = jnp.where(rank_v[d:d + 1, :] == slot, 1.0, 0.0)
@@ -85,6 +86,7 @@
     stack = jnp.concatenate([rank0, rank1, jnp.broadcast_to(ids0.astype(F32), (16, tok)),
                              jnp.broadcast_to(ids1.astype(F32), (16, tok)), jnp.zeros((64, tok), F32)], axis=0)
     cols_v[...] = stack.T
+    loads[2].wait()
     logits = dot_nt(x_v[...], wgt_ref[...])
     lane8 = lax.broadcasted_iota(jnp.int32, (tok, N_DEV), 1).astype(F32)
     sel0 = jnp.sum(jnp.where(lane8 == cols_v[:, 32:33], logits, 0.0), axis=1, keepdims=True)
@@ -94,7 +96,7 @@
     e1 = jnp.exp(sel1 - top)
     gate_v[0] = e0 / (e0 + e1)
     gate_v[1] = e1 / (e0 + e1)
-    loads[1].wait()
+    loads[3].wait()
     dout_f = dout_v[...].astype(F32)
     dyflat_v[0:tok, :] = (gate_v[0] * dout_f).astype(BF16)
     dyflat_v[tok:2 * tok, :] = (gate_v[1] * dout_f).astype(BF16)
@@ -107,8 +109,8 @@
             remote(1, sdy, rdy, d).start()
 
     hid = 512
-    loads[2].wait()
-    loads[3].wait()
+    loads[4].wait()
+    loads[5].wait()
     for c in range(4):
         for d in (2 * c, 2 * c + 1):
             if d:
@@ -206,25 +208,41 @@
         remote(3, sdx, rdx, d).start()
     acc = dot_nn(d_log, wgt_ref[...])
 
-    for c in range(4):
+    for c in range(3):
         for d in (2 * c, 2 * c + 1):
             if d:
                 remote(3, sdx, rdx, d).wait_recv()
         span = slice(2 * ROWS * c, 2 * ROWS * (c + 1))
         acc = acc + dot_nn(q0_v[:, span] + q1_v[:, span], rdx[span])
-    gx_ref[...] = acc.astype(BF16)
+    acc_ref[...] = acc
+    span = slice(6 * ROWS, 8 * ROWS)
+    qlast_ref[...] = q0_v[:, span] + q1_v[:, span]
     for d in range(1, N_DEV):
         wg_copy(d).wait_recv()
     total = wg_all[0]
     for s in range(1, N_DEV):
         total = total + wg_all[s]
     gwg_ref[...] = total
+    for d in (6, 7):
+        remote(3, sdx, rdx, d).wait_recv()
     for d in range(1, N_DEV):
         remote(0, sx, rx, d).wait_send()
         remote(1, sdy, rdy, d).wait_send()
         remote(2, sy, ry, d).wait_send()
         remote(3, sdx, rdx, d).wait_send()
         wg_copy(d).wait_send()
+
+
+def finish_kernel(out_v, gwin_v, gwout_v, gwg_v, acc_v, qlast_v, dx_v,
+                  out_hbm, gx_hbm, gwin_hbm, gwout_hbm, gwg_hbm, gx_v, sem):
+    stores = [pltpu.make_async_copy(src, dst, sem.at[i]) for i, (src, dst) in enumerate(
+        ((gwin_v, gwin_hbm), (gwout_v, gwout_hbm), (out_v, out_hbm), (gwg_v, gwg_hbm), (gx_v, gx_hbm)))]
+    for st in stores[:4]:
+        st.start()
+    gx_v[...] = (acc_v[...] + dot_nn(qlast_v[...], dx_v[6 * ROWS:8 * ROWS])).astype(BF16)
+    stores[4].start()
+    for st in stores:
+        st.wait()
 
 
 def local_block(tokens, grad_out, expert_ids, w_gate, w_in, w_out):
@@ -235,28 +253,42 @@
     vmem = pl.BlockSpec(memory_space=pltpu.VMEM)
     hbm = pl.BlockSpec(memory_space=pl.ANY)
     blocks = pltpu.VMEM((slots, d_model), BF16)
-    out, gx, gwin, gwout, gwg = pl.pallas_call(
+    args = [pltpu.with_memory_space_constraint(a, pltpu.HBM)
+            for a in (expert_ids.T, w_gate.T, tokens, grad_out, w_in[0], w_out[0])]
+    kept = pl.pallas_call(
         moe_kernel,
-        out_shape=(jax.ShapeDtypeStruct((tok, d_model), BF16), jax.ShapeDtypeStruct((tok, d_model), BF16),
-                   jax.ShapeDtypeStruct((d_model, d_hid), F32), jax.ShapeDtypeStruct((d_hid, d_model), F32),
-                   jax.ShapeDtypeStruct((n_exp, d_model), F32)),
-        in_specs=[vmem, vmem, hbm, hbm, hbm, hbm],
-        out_specs=(vmem,) * 5,
+        out_shape=(pltpu.VMEM((tok, d_model), BF16), pltpu.VMEM((d_model, d_hid), F32), pltpu.VMEM((d_hid, d_model), F32),
+                   pltpu.VMEM((n_exp, d_model), F32), pltpu.VMEM((tok, d_model), F32),
+                   pltpu.VMEM((tok, 2 * ROWS), BF16), pltpu.VMEM((slots, d_model), BF16)),
+        in_specs=[hbm] * 6,
+        out_specs=(vmem,) * 7,
         scratch_shapes=[
+            pltpu.VMEM((2, tok), jnp.int32), pltpu.VMEM((n_exp, d_model), BF16),
             pltpu.VMEM((tok, d_model), BF16), pltpu.VMEM((tok, d_model), BF16),
             pltpu.VMEM((d_model, d_hid), BF16), pltpu.VMEM((d_hid, d_model), BF16),
             pltpu.VMEM((32, tok), F32), pltpu.VMEM((n_exp, ROWS, 2 * tok), BF16),
             pltpu.VMEM((tok, slots), BF16), pltpu.VMEM((tok, slots), BF16),
             pltpu.VMEM((2 * tok, d_model), BF16), pltpu.VMEM((2, tok, 1), F32), pltpu.VMEM((tok, 128), F32),
-            blocks, blocks, blocks, blocks, blocks, blocks, blocks, blocks,
+            blocks, blocks, blocks, blocks, blocks, blocks, blocks,
             pltpu.VMEM((slots, d_hid), BF16), pltpu.VMEM((slots, d_hid), F32), pltpu.VMEM((slots, d_hid), BF16),
             pltpu.VMEM((d_model, slots), BF16), pltpu.VMEM((n_exp, d_model), F32), pltpu.VMEM((n_exp, n_exp, d_model), F32),
-            pltpu.SemaphoreType.DMA((4,)), pltpu.SemaphoreType.DMA((4, n_exp)), pltpu.SemaphoreType.DMA((4, n_exp)),
+            pltpu.SemaphoreType.DMA((6,)), pltpu.SemaphoreType.DMA((4, n_exp)), pltpu.SemaphoreType.DMA((4, n_exp)),
             pltpu.SemaphoreType.DMA((n_exp,)), pltpu.SemaphoreType.DMA((n_exp,)),
         ],
-        compiler_params=pltpu.CompilerParams(collective_id=0, has_side_effects=True, vmem_limit_bytes=47 * 1024 * 1024),
+        compiler_params=pltpu.CompilerParams(collective_id=0, has_side_effects=True, vmem_limit_bytes=46 * 1024 * 1024),
         name='moe_step',
-    )(expert_ids.T, w_gate.T, tokens, grad_out, w_in[0], w_out[0])
+    )(*args)
+    out, gx, gwin, gwout, gwg = pl.pallas_call(
+        finish_kernel,
+        out_shape=(jax.ShapeDtypeStruct((tok, d_model), BF16), jax.ShapeDtypeStruct((tok, d_model), BF16),
+                   jax.ShapeDtypeStruct((d_model, d_hid), F32), jax.ShapeDtypeStruct((d_hid, d_model), F32),
+                   jax.ShapeDtypeStruct((n_exp, d_model), F32)),
+        in_specs=[vmem] * 7,
+        out_specs=(hbm,) * 5,
+        scratch_shapes=[pltpu.VMEM((tok, d_model), BF16), pltpu.SemaphoreType.DMA((5,))],
+        compiler_params=pltpu.CompilerParams(vmem_limit_bytes=16 * 1024 * 1024),
+        name='moe_finish',
+    )(*kept)
     return out, gx, gwin[None], gwout[None], gwg.T
 
 

time: 73.5 us -> 57.9 us (0.79)
  local copies, waits for them, and re-layouts: 15.7 us -> 0 us
    unnamed x19 -> x0, local copies, waits for them, and re-layouts: 15.7 us -> none
    pallas_call x1 -> x2, Pallas kernels: 56.8 us -> 57 us  [the longest x1 53.3 us: local_block(): pl.pallas_call(moe_kernel, out_shape=(pltpu.VMEM((tok, d_model), BF16), p...]
where the time goes in v2:
time: 57.9 us; the launch traced here: 57.8 us
  Pallas kernels  57 us (98%)
  between operations  0.8 us (1%)
    pallas_call x1, Pallas kernels, local_block(): pl.pallas_call(moe_kernel, out_shape=(pltpu.VMEM((tok, d_model), BF16), p...  53.3 us
    pallas_call x1, Pallas kernels, local_block(): pl.pallas_call(finish_kernel, out_shape=(jax.ShapeDtypeStruct((tok, d_mod...  3.66 us

profile of v2, /device:TPU:0, one launch (start us, length us, event | category | flops | bytes accessed | tf_op | source)
XLA Modules:
  0.0 57.8 jit_solution(4400756737220777368)
XLA Ops:
  0.6 53.3 %moe_step.1 = (bf16[512,512]{1,0:T(8,128)(2,1)S(1)}, f32[512,2048]{1,0:T(8,128)S(1)}, f32[2048,512]{1,0:T(8,128)S(1)}, f32[8,512]{1,0:T(8,128)S(1)}, f32[512,512...) custom-call(s32[2,512]{1,0:T(2,128)} %bitcast.10, bf16[8,512]{1,0:T(8,128)(2,1)} %bitcast.9, ...), custom_call_target="tpu_custom_call" | custom-call | tf_op jit(solution)/shard_map/moe_step/pallas_call | solution.py:258
  54.0 3.7 %moe_finish.1 = (bf16[512,512]{1,0:T(8,128)(2,1)}, bf16[512,512]{1,0:T(8,128)(2,1)}, f32[512,2048]{1,0:T(8,128)}, f32[2048,512]{1,0:T(8,128)}, f32[8,512]{1,0:T(8,128)}) custom-call(bf16[512,512]{1,0:T(8,128)(2,1)S(1)} %get-tuple-element.17.out_v, f32[512,2048]{1,0:T(8,128)S(1)} %get-tuple-element.18.gwin_v, f32[2048,512]{1,0:T(8,128)S(1)} %get-tuple-element.19.gwout_v, ...), custom_call_target="tpu_custom_call" | custom-call | tf_op jit(solution)/shard_map/moe_finish/pallas_call | solution.py:281

commit v3 on v2

--- a/solution.py
+++ b/solution.py
@@ -31,10 +31,11 @@
 def moe_kernel(ids_hbm, wgt_hbm, x_hbm, dout_hbm, win_hbm, wout_hbm,
                out_ref, gwin_ref, gwout_ref, gwg_ref, acc_ref, qlast_ref, rdx,
                ids_ref, wgt_ref, x_v, dout_v, win_v, wout_v, rank_v, p_v, q0_v, q1_v, dyflat_v, gate_v, cols_v,
-               sx, rx, sdy, rdy, sy, ry, sdx, h_v, gp_v, da_v, xt_v, wg_part, wg_all,
+               sx, rx, sdy, rdy, sy, ry, sdx, h_v, gp_v, da_v, xt_v, before_v, wg_part, wg_mate, wg_chip,
                load_sem, send_sem, recv_sem, wg_send, wg_recv):
     tok = x_v.shape[0]
     d_hid = win_v.shape[1]
+    half = x_v.shape[1] // 2
     me = lax.axis_index('ep')
     core, col, row = me % 2, (me // 2) % 2, me // 4
 
@@ -55,22 +56,21 @@
         ld.start()
 
     rel = lax.broadcasted_iota(jnp.int32, (16, tok), 0) ^ me
+    before_v[...] = jnp.where(lax.broadcasted_iota(jnp.int32, (tok, tok), 0) < lax.broadcasted_iota(jnp.int32, (tok, tok), 1), 1.0, 0.0).astype(BF16)
+    slot = lax.broadcasted_iota(jnp.int32, (ROWS, tok), 0).astype(F32)
     loads[0].wait()
     ids0 = ids_ref[0:1, :]
     ids1 = ids_ref[1:2, :]
     hit0 = rel == ids0
     hit1 = rel == ids1
     hot = jnp.where(hit0 | hit1, 1.0, 0.0).astype(BF16)
-    before = jnp.where(lax.broadcasted_iota(jnp.int32, (tok, tok), 0) < lax.broadcasted_iota(jnp.int32, (tok, tok), 1), 1.0, 0.0).astype(BF16)
-    rank = dot_nn(hot, before)
+    rank = dot_nn(hot, before_v[...])
     rank0 = jnp.where(hit0, rank, -1.0)
     rank1 = jnp.where(hit1, rank, -1.0)
     rank_v[0:16, :] = rank0
     rank_v[16:32, :] = rank1
-    slot = lax.broadcasted_iota(jnp.int32, (ROWS, tok), 0).astype(F32)
 
     loads[1].wait()
-    pl.semaphore_wait(barrier, N_DEV - 1)
     for d in (2, 4, 3, 5, 6, 7, 1, 0):
         pick0 = jnp.where(rank_v[d:d + 1, :] == slot, 1.0, 0.0)
         pick1 = jnp.where(rank_v[16 + d:17 + d, :] == slot, 1.0, 0.0)
@@ -79,6 +79,8 @@
             rx[0:ROWS] = block
         else:
             sx[d * ROWS:(d + 1) * ROWS] = block
+            if d == 2:
+                pl.semaphore_wait(barrier, N_DEV - 1)
             remote(0, sx, rx, d).start()
         p_v[d, :, 0:tok] = pick0.astype(BF16)
         p_v[d, :, tok:2 * tok] = pick1.astype(BF16)
@@ -164,7 +166,7 @@
                 rdx[0:ROWS] = block
             else:
                 sdx[d * ROWS:(d + 1) * ROWS] = block
-                if c < 3:
+                if c in (0, 3):
                     remote(3, sdx, rdx, d).start()
 
     for c in range(4):
@@ -194,53 +196,68 @@
     mean = g0 * dg0 + g1 * dg1
     d_log = (jnp.where(lane8 == cols_v[:, 32:33], g0 * (dg0 - mean), 0.0)
              + jnp.where(lane8 == cols_v[:, 48:49], g1 * (dg1 - mean), 0.0)).astype(BF16)
-    wg_part[...] = dot_tn(d_log, x_v[...])
-    wg_all[me] = wg_part[...]
-
-    def wg_copy(d):
+    for i in range(2):
+        wg_part[i] = dot_tn(d_log, x_v[:, i * half:(i + 1) * half])
+
+    def wg_copy(i, src, dst, d):
         return pltpu.make_async_remote_copy(
-            src_ref=wg_part, dst_ref=wg_all.at[me], send_sem=wg_send.at[d], recv_sem=wg_recv.at[d],
+            src_ref=src, dst_ref=dst, send_sem=wg_send.at[i], recv_sem=wg_recv.at[i],
             device_id=(peer(d),), device_id_type=MESH)
 
-    for d in range(1, N_DEV):
-        wg_copy(d).start()
-    for d in (6, 7):
+    chip = 2 * row + col
+    to_mate = wg_copy(0, wg_part.at[1 - core], wg_mate, 1)
+    to_mate.start()
+    acc = dot_nn(d_log, wgt_ref[...])
+    to_mate.wait_recv()
+    wg_chip[chip] = wg_part[core] + wg_mate[...]
+    to_chips = [wg_copy(1 + i, wg_chip.at[chip], wg_chip.at[chip], 2 * (i + 1)) for i in range(3)]
+    for cp in to_chips:
+        cp.start()
+    for d in (2, 4, 3, 5):
         remote(3, sdx, rdx, d).start()
-    acc = dot_nn(d_log, wgt_ref[...])
-
-    for c in range(3):
+
+    for c in (0, 3):
         for d in (2 * c, 2 * c + 1):
             if d:
                 remote(3, sdx, rdx, d).wait_recv()
         span = slice(2 * ROWS * c, 2 * ROWS * (c + 1))
         acc = acc + dot_nn(q0_v[:, span] + q1_v[:, span], rdx[span])
     acc_ref[...] = acc
-    span = slice(6 * ROWS, 8 * ROWS)
+    span = slice(2 * ROWS, 6 * ROWS)
     qlast_ref[...] = q0_v[:, span] + q1_v[:, span]
-    for d in range(1, N_DEV):
-        wg_copy(d).wait_recv()
-    total = wg_all[0]
-    for s in range(1, N_DEV):
-        total = total + wg_all[s]
-    gwg_ref[...] = total
-    for d in (6, 7):
-        remote(3, sdx, rdx, d).wait_recv()
+    for cp in to_chips:
+        cp.wait_recv()
+    gwg_ref[core] = (wg_chip[0] + wg_chip[1]) + (wg_chip[2] + wg_chip[3])
+    swap = wg_copy(4, gwg_ref.at[core], gwg_ref.at[core], 1)
+    swap.start()
+    to_mate.wait_send()
     for d in range(1, N_DEV):
         remote(0, sx, rx, d).wait_send()
         remote(1, sdy, rdy, d).wait_send()
         remote(2, sy, ry, d).wait_send()
+    for cp in to_chips:
+        cp.wait_send()
+    swap.wait()
+    for d in (2, 4, 3, 5):
+        remote(3, sdx, rdx, d).wait_recv()
+    for d in range(1, N_DEV):
         remote(3, sdx, rdx, d).wait_send()
-        wg_copy(d).wait_send()
 
 
 def finish_kernel(out_v, gwin_v, gwout_v, gwg_v, acc_v, qlast_v, dx_v,
                   out_hbm, gx_hbm, gwin_hbm, gwout_hbm, gwg_hbm, gx_v, sem):
-    stores = [pltpu.make_async_copy(src, dst, sem.at[i]) for i, (src, dst) in enumerate(
-        ((gwin_v, gwin_hbm), (gwout_v, gwout_hbm), (out_v, out_hbm), (gwg_v, gwg_hbm), (gx_v, gx_hbm)))]
-    for st in stores[:4]:
+    pieces = []
+    for src, dst in ((gwin_v, gwin_hbm), (gwout_v, gwout_hbm)):
+        n = src.shape[0] // 4
+        pieces += [(src.at[pl.ds(i * n, n)], dst.at[pl.ds(i * n, n)]) for i in range(4)]
+    half = gwg_v.shape[2]
+    pieces += [(out_v, out_hbm), (gwg_v.at[0], gwg_hbm.at[:, pl.ds(0, half)]), (gwg_v.at[1], gwg_hbm.at[:, pl.ds(half, half)]),
+               (gx_v, gx_hbm)]
+    stores = [pltpu.make_async_copy(src, dst, sem.at[i]) for i, (src, dst) in enumerate(pieces)]
+    for st in stores[:-1]:
         st.start()
-    gx_v[...] = (acc_v[...] + dot_nn(qlast_v[...], dx_v[6 * ROWS:8 * ROWS])).astype(BF16)
-    stores[4].start()
+    gx_v[...] = (acc_v[...] + dot_nn(qlast_v[...], dx_v[2 * ROWS:6 * ROWS])).astype(BF16)
+    stores[-1].start()
     for st in stores:
         st.wait()
 
@@ -258,8 +275,8 @@
     kept = pl.pallas_call(
         moe_kernel,
         out_shape=(pltpu.VMEM((tok, d_model), BF16), pltpu.VMEM((d_model, d_hid), F32), pltpu.VMEM((d_hid, d_model), F32),
-                   pltpu.VMEM((n_exp, d_model), F32), pltpu.VMEM((tok, d_model), F32),
-                   pltpu.VMEM((tok, 2 * ROWS), BF16), pltpu.VMEM((slots, d_model), BF16)),
+                   pltpu.VMEM((2, n_exp, d_model // 2), F32), pltpu.VMEM((tok, d_model), F32),
+                   pltpu.VMEM((tok, 4 * ROWS), BF16), pltpu.VMEM((slots, d_model), BF16)),
         in_specs=[hbm] * 6,
         out_specs=(vmem,) * 7,
         scratch_shapes=[
@@ -271,9 +288,10 @@
             pltpu.VMEM((2 * tok, d_model), BF16), pltpu.VMEM((2, tok, 1), F32), pltpu.VMEM((tok, 128), F32),
             blocks, blocks, blocks, blocks, blocks, blocks, blocks,
             pltpu.VMEM((slots, d_hid), BF16), pltpu.VMEM((slots, d_hid), F32), pltpu.VMEM((slots, d_hid), BF16),
-            pltpu.VMEM((d_model, slots), BF16), pltpu.VMEM((n_exp, d_model), F32), pltpu.VMEM((n_exp, n_exp, d_model), F32),
+            pltpu.VMEM((d_model, slots), BF16), pltpu.VMEM((tok, tok), BF16),
+            pltpu.VMEM((2, n_exp, d_model // 2), F32), pltpu.VMEM((n_exp, d_model // 2), F32), pltpu.VMEM((4, n_exp, d_model // 2), F32),
             pltpu.SemaphoreType.DMA((6,)), pltpu.SemaphoreType.DMA((4, n_exp)), pltpu.SemaphoreType.DMA((4, n_exp)),
-            pltpu.SemaphoreType.DMA((n_exp,)), pltpu.SemaphoreType.DMA((n_exp,)),
+            pltpu.SemaphoreType.DMA((5,)), pltpu.SemaphoreType.DMA((5,)),
         ],
         compiler_params=pltpu.CompilerParams(collective_id=0, has_side_effects=True, vmem_limit_bytes=46 * 1024 * 1024),
         name='moe_step',
@@ -285,7 +303,7 @@
                    jax.ShapeDtypeStruct((n_exp, d_model), F32)),
         in_specs=[vmem] * 7,
         out_specs=(hbm,) * 5,
-        scratch_shapes=[pltpu.VMEM((tok, d_model), BF16), pltpu.SemaphoreType.DMA((5,))],
+        scratch_shapes=[pltpu.VMEM((tok, d_model), BF16), pltpu.SemaphoreType.DMA((12,))],
         compiler_params=pltpu.CompilerParams(vmem_limit_bytes=16 * 1024 * 1024),
         name='moe_finish',
     )(*kept)

time: 57.9 us -> 59.9 us (1.035)
  Pallas kernels: 57 us -> 58.7 us
    pallas_call x1, Pallas kernels: 53.3 us -> 54.9 us  [local_block(): pl.pallas_call(moe_kernel, out_shape=(pltpu.VMEM((tok, d_model), BF16), p...]
where the time goes in v3:
time: 59.9 us; the launch traced here: 59.5 us
  Pallas kernels  58.7 us (98%)
  between operations  0.8 us (1%)
    pallas_call x1, Pallas kernels, local_block(): pl.pallas_call(moe_kernel, out_shape=(pltpu.VMEM((tok, d_model), BF16), p...  54.9 us
    pallas_call x1, Pallas kernels, local_block(): pl.pallas_call(finish_kernel, out_shape=(jax.ShapeDtypeStruct((tok, d_mod...  3.73 us

profile of v3, /device:TPU:0, one launch (start us, length us, event | category | flops | bytes accessed | tf_op | source)
XLA Modules:
  0.0 59.5 jit_solution(13780443959793908088)
XLA Ops:
  0.6 54.9 %moe_step.1 = (bf16[512,512]{1,0:T(8,128)(2,1)S(1)}, f32[512,2048]{1,0:T(8,128)S(1)}, f32[2048,512]{1,0:T(8,128)S(1)}, f32[2,8,256]{2,1,0:T(8,128)S(1)}, f32[512...) custom-call(s32[2,512]{1,0:T(2,128)} %bitcast.10, bf16[8,512]{1,0:T(8,128)(2,1)} %bitcast.9, ...), custom_call_target="tpu_custom_call" | custom-call | tf_op jit(solution)/shard_map/moe_step/pallas_call | solution.py:275
  55.6 3.7 %moe_finish.1 = (bf16[512,512]{1,0:T(8,128)(2,1)}, bf16[512,512]{1,0:T(8,128)(2,1)}, f32[512,2048]{1,0:T(8,128)}, f32[2048,512]{1,0:T(8,128)}, f32[8,512]{1,0:T(8,128)}) custom-call(bf16[512,512]{1,0:T(8,128)(2,1)S(1)} %get-tuple-element.17.out_v, f32[512,2048]{1,0:T(8,128)S(1)} %get-tuple-element.18.gwin_v, f32[2048,512]{1,0:T(8,128)S(1)} %get-tuple-element.19.gwout_v, ...), custom_call_target="tpu_custom_call" | custom-call | tf_op jit(solution)/shard_map/moe_finish/pallas_call | solution.py:299

commit v4 on v3

--- a/solution.py
+++ b/solution.py
@@ -8,6 +8,8 @@
 from jax.sharding import PartitionSpec as P
 
 N_DEV = 8
+DX_EARLY = (6, 2, 4, 7)
+DX_LATE = (3, 5)
 ROWS = 128
 MESH = pl.DeviceIdType.MESH
 F32 = jnp.float32
@@ -166,11 +168,13 @@
                 rdx[0:ROWS] = block
             else:
                 sdx[d * ROWS:(d + 1) * ROWS] = block
-                if c in (0, 3):
+                if c == 0:
                     remote(3, sdx, rdx, d).start()
 
     for c in range(4):
         bwd_chunk(c)
+    for d in DX_EARLY:
+        remote(3, sdx, rdx, d).start()
 
     xt_v[...] = rx[...].T
     wt = 256
@@ -183,14 +187,19 @@
 
     lax.fori_loop(0, d_hid // wt, grad_tile, 0)
 
-    for d in range(1, N_DEV):
+    for d in range(1, 6):
         remote(2, sy, ry, d).wait_recv()
-    y0 = dot_nn(q0_v[...], ry[...])
-    y1 = dot_nn(q1_v[...], ry[...])
+    span = slice(0, 6 * ROWS)
+    y0 = dot_nn(q0_v[:, span], ry[span])
+    y1 = dot_nn(q1_v[:, span], ry[span])
+    for d in (6, 7):
+        remote(2, sy, ry, d).wait_recv()
+    span = slice(6 * ROWS, 8 * ROWS)
+    y0 = y0 + dot_nn(q0_v[:, span], ry[span])
+    y1 = y1 + dot_nn(q1_v[:, span], ry[span])
     g0 = gate_v[0]
     g1 = gate_v[1]
     dout_f = dout_v[...].astype(F32)
-    out_ref[...] = (g0 * y0 + g1 * y1).astype(BF16)
     dg0 = jnp.sum(dout_f * y0, axis=1, keepdims=True)
     dg1 = jnp.sum(dout_f * y1, axis=1, keepdims=True)
     mean = g0 * dg0 + g1 * dg1
@@ -207,13 +216,14 @@
     chip = 2 * row + col
     to_mate = wg_copy(0, wg_part.at[1 - core], wg_mate, 1)
     to_mate.start()
+    out_ref[...] = (g0 * y0 + g1 * y1).astype(BF16)
     acc = dot_nn(d_log, wgt_ref[...])
     to_mate.wait_recv()
     wg_chip[chip] = wg_part[core] + wg_mate[...]
     to_chips = [wg_copy(1 + i, wg_chip.at[chip], wg_chip.at[chip], 2 * (i + 1)) for i in range(3)]
     for cp in to_chips:
         cp.start()
-    for d in (2, 4, 3, 5):
+    for d in DX_LATE:
         remote(3, sdx, rdx, d).start()
 
     for c in (0, 3):
@@ -246,13 +256,9 @@
 
 def finish_kernel(out_v, gwin_v, gwout_v, gwg_v, acc_v, qlast_v, dx_v,
                   out_hbm, gx_hbm, gwin_hbm, gwout_hbm, gwg_hbm, gx_v, sem):
-    pieces = []
-    for src, dst in ((gwin_v, gwin_hbm), (gwout_v, gwout_hbm)):
-        n = src.shape[0] // 4
-        pieces += [(src.at[pl.ds(i * n, n)], dst.at[pl.ds(i * n, n)]) for i in range(4)]
     half = gwg_v.shape[2]
-    pieces += [(out_v, out_hbm), (gwg_v.at[0], gwg_hbm.at[:, pl.ds(0, half)]), (gwg_v.at[1], gwg_hbm.at[:, pl.ds(half, half)]),
-               (gx_v, gx_hbm)]
+    pieces = [(gwin_v, gwin_hbm), (gwout_v, gwout_hbm), (out_v, out_hbm), (gwg_v.at[0], gwg_hbm.at[:, pl.ds(0, half)]),
+              (gwg_v.at[1], gwg_hbm.at[:, pl.ds(half, half)]), (gx_v, gx_hbm)]
     stores = [pltpu.make_async_copy(src, dst, sem.at[i]) for i, (src, dst) in enumerate(pieces)]
     for st in stores[:-1]:
         st.start()
@@ -303,7 +309,7 @@
                    jax.ShapeDtypeStruct((n_exp, d_model), F32)),
         in_specs=[vmem] * 7,
         out_specs=(hbm,) * 5,
-        scratch_shapes=[pltpu.VMEM((tok, d_model), BF16), pltpu.SemaphoreType.DMA((12,))],
+        scratch_shapes=[pltpu.VMEM((tok, d_model), BF16), pltpu.SemaphoreType.DMA((6,))],
         compiler_params=pltpu.CompilerParams(vmem_limit_bytes=16 * 1024 * 1024),
         name='moe_finish',
     )(*kept)

time: 59.9 us -> 56.5 us (0.943)
  Pallas kernels: 58.7 us -> 55.6 us
    pallas_call x1, Pallas kernels: 54.9 us -> 51.9 us  [local_block(): pl.pallas_call(moe_kernel, out_shape=(pltpu.VMEM((tok, d_model), BF16), p...]
where the time goes in v4:
time: 56.5 us; the launch traced here: 56.4 us
  Pallas kernels  55.6 us (98%)
  between operations  0.8 us (1%)
    pallas_call x1, Pallas kernels, local_block(): pl.pallas_call(moe_kernel, out_shape=(pltpu.VMEM((tok, d_model), BF16), p...  51.9 us
    pallas_call x1, Pallas kernels, local_block(): pl.pallas_call(finish_kernel, out_shape=(jax.ShapeDtypeStruct((tok, d_mod...  3.67 us

profile of v4, /device:TPU:0, one launch (start us, length us, event | category | flops | bytes accessed | tf_op | source)
XLA Modules:
  0.0 56.4 jit_solution(14294517379004018294)
XLA Ops:
  0.6 51.9 %moe_step.1 = (bf16[512,512]{1,0:T(8,128)(2,1)S(1)}, f32[512,2048]{1,0:T(8,128)S(1)}, f32[2048,512]{1,0:T(8,128)S(1)}, f32[2,8,256]{2,1,0:T(8,128)S(1)}, f32[512...) custom-call(s32[2,512]{1,0:T(2,128)} %bitcast.10, bf16[8,512]{1,0:T(8,128)(2,1)} %bitcast.9, ...), custom_call_target="tpu_custom_call" | custom-call | tf_op jit(solution)/shard_map/moe_step/pallas_call | solution.py:281
  52.5 3.7 %moe_finish.1 = (bf16[512,512]{1,0:T(8,128)(2,1)}, bf16[512,512]{1,0:T(8,128)(2,1)}, f32[512,2048]{1,0:T(8,128)}, f32[2048,512]{1,0:T(8,128)}, f32[8,512]{1,0:T(8,128)}) custom-call(bf16[512,512]{1,0:T(8,128)(2,1)S(1)} %get-tuple-element.17.out_v, f32[512,2048]{1,0:T(8,128)S(1)} %get-tuple-element.18.gwin_v, f32[2048,512]{1,0:T(8,128)S(1)} %get-tuple-element.19.gwout_v, ...), custom_call_target="tpu_custom_call" | custom-call | tf_op jit(solution)/shard_map/moe_finish/pallas_call | solution.py:305

commit v5 on v4

--- a/solution.py
+++ b/solution.py
@@ -8,8 +8,8 @@
 from jax.sharding import PartitionSpec as P
 
 N_DEV = 8
-DX_EARLY = (6, 2, 4, 7)
-DX_LATE = (3, 5)
+DX_EARLY = (1, 2, 4, 6, 3, 5)
+DX_LATE = (7,)
 ROWS = 128
 MESH = pl.DeviceIdType.MESH
 F32 = jnp.float32
@@ -31,7 +31,7 @@
 
 
 def moe_kernel(ids_hbm, wgt_hbm, x_hbm, dout_hbm, win_hbm, wout_hbm,
-               out_ref, gwin_ref, gwout_ref, gwg_ref, acc_ref, qlast_ref, rdx,
+               out_ref, gwin_ref, gwout_ref, gwg_ref, acc_ref, q01_ref, rdx,
                ids_ref, wgt_ref, x_v, dout_v, win_v, wout_v, rank_v, p_v, q0_v, q1_v, dyflat_v, gate_v, cols_v,
                sx, rx, sdy, rdy, sy, ry, sdx, h_v, gp_v, da_v, xt_v, before_v, wg_part, wg_mate, wg_chip,
                load_sem, send_sem, recv_sem, wg_send, wg_recv):
@@ -58,7 +58,8 @@
         ld.start()
 
     rel = lax.broadcasted_iota(jnp.int32, (16, tok), 0) ^ me
-    before_v[...] = jnp.where(lax.broadcasted_iota(jnp.int32, (tok, tok), 0) < lax.broadcasted_iota(jnp.int32, (tok, tok), 1), 1.0, 0.0).astype(BF16)
+    lane2 = lax.broadcasted_iota(jnp.int32, (ROWS, 2 * ROWS), 1)
+    before_v[...] = jnp.where((lax.broadcasted_iota(jnp.int32, (ROWS, 2 * ROWS), 0) < lane2) | (lane2 >= ROWS), 1.0, 0.0).astype(BF16)
     slot = lax.broadcasted_iota(jnp.int32, (ROWS, tok), 0).astype(F32)
     loads[0].wait()
     ids0 = ids_ref[0:1, :]
@@ -66,7 +67,14 @@
     hit0 = rel == ids0
     hit1 = rel == ids1
     hot = jnp.where(hit0 | hit1, 1.0, 0.0).astype(BF16)
-    rank = dot_nn(hot, before_v[...])
+    groups = [slice(g * ROWS, (g + 1) * ROWS) for g in range(tok // ROWS)]
+    counts = dot_nn(jnp.concatenate([hot[:, g] for g in groups], axis=0), before_v[...])
+    rank, base = [], 0.0
+    for g in range(tok // ROWS):
+        part = counts[16 * g:16 * (g + 1)]
+        rank.append(part[:, 0:ROWS] + base)
+        base = base + part[:, ROWS:2 * ROWS]
+    rank = jnp.concatenate(rank, axis=1)
     rank0 = jnp.where(hit0, rank, -1.0)
     rank1 = jnp.where(hit1, rank, -1.0)
     rank_v[0:16, :] = rank0
@@ -115,14 +123,16 @@
     hid = 512
     loads[4].wait()
     loads[5].wait()
-    for c in range(4):
-        for d in (2 * c, 2 * c + 1):
-            if d:
-                remote(0, sx, rx, d).wait_recv()
-        rows = slice(2 * ROWS * c, 2 * ROWS * (c + 1))
+    def fwd_chunk(c, carry):
+        @pl.when(c > 0)
+        def _():
+            remote(0, sx, rx, 2 * c).wait_recv()
+
+        remote(0, sx, rx, 2 * c + 1).wait_recv()
+        rows = pl.ds(pl.multiple_of(c * (2 * ROWS), 2 * ROWS), 2 * ROWS)
         x_c = rx[rows]
 
-        def fwd_tile(j, carry):
+        def fwd_tile(j, inner):
             cols = pl.ds(pl.multiple_of(j * hid, hid), hid)
             a = dot_nn(x_c, win_v[:, cols])
             sq = a * a
@@ -130,49 +140,51 @@
             cdf = 0.5 * (1.0 + t)
             h_v[rows, cols] = (a * cdf).astype(BF16)
             gp_v[rows, cols] = cdf + (0.5 * a) * (1.0 - t * t) * (SQRT_2_PI * (1.0 + (3.0 * CUBIC) * sq))
-            return carry
+            return inner
 
         lax.fori_loop(0, d_hid // hid, fwd_tile, 0)
-        y_c = dot_nn(h_v[rows, :], wout_v[...]).astype(BF16)
-        for i, d in enumerate((2 * c, 2 * c + 1)):
-            block = y_c[i * ROWS:(i + 1) * ROWS]
-            if d == 0:
-                ry[0:ROWS] = block
-            else:
-                sy[d * ROWS:(d + 1) * ROWS] = block
-                remote(2, sy, ry, d).start()
+        sy[rows] = dot_nn(h_v[rows], wout_v[...]).astype(BF16)
+
+        @pl.when(c > 0)
+        def _():
+            remote(2, sy, ry, 2 * c).start()
+
+        remote(2, sy, ry, 2 * c + 1).start()
+        return carry
+
+    lax.fori_loop(0, N_DEV // 2, fwd_chunk, 0)
+    ry[0:ROWS] = sy[0:ROWS]
 
     slot_l = lax.broadcasted_iota(jnp.int32, (tok, ROWS), 1).astype(F32)
     for d in range(N_DEV):
-        q0_v[:, d * ROWS:(d + 1) * ROWS] = jnp.where(cols_v[:, d:d + 1] == slot_l, 1.0, 0.0).astype(BF16)
-        q1_v[:, d * ROWS:(d + 1) * ROWS] = jnp.where(cols_v[:, 16 + d:17 + d] == slot_l, 1.0, 0.0).astype(BF16)
-
-    def bwd_chunk(c):
-        for d in (2 * c, 2 * c + 1):
-            if d:
-                remote(1, sdy, rdy, d).wait_recv()
-        rows = slice(2 * ROWS * c, 2 * ROWS * (c + 1))
+        span = slice(d * ROWS, (d + 1) * ROWS)
+        own0 = jnp.where(cols_v[:, d:d + 1] == slot_l, 1.0, 0.0)
+        own1 = jnp.where(cols_v[:, 16 + d:17 + d] == slot_l, 1.0, 0.0)
+        q0_v[:, span] = own0.astype(BF16)
+        q1_v[:, span] = own1.astype(BF16)
+        q01_ref[:, span] = (own0 + own1).astype(BF16)
+
+    def bwd_chunk(c, carry):
+        @pl.when(c > 0)
+        def _():
+            remote(1, sdy, rdy, 2 * c).wait_recv()
+
+        remote(1, sdy, rdy, 2 * c + 1).wait_recv()
+        rows = pl.ds(pl.multiple_of(c * (2 * ROWS), 2 * ROWS), 2 * ROWS)
         dy_c = rdy[rows]
 
-        def bwd_tile(j, carry):
+        def bwd_tile(j, inner):
             cols = pl.ds(pl.multiple_of(j * hid, hid), hid)
             dh = dot_nt(dy_c, wout_v[cols, :])
             da_v[rows, cols] = (dh * gp_v[rows, cols]).astype(BF16)
-            return carry
+            return inner
 
         lax.fori_loop(0, d_hid // hid, bwd_tile, 0)
-        dx_c = dot_nt(da_v[rows, :], win_v[...]).astype(BF16)
-        for i, d in enumerate((2 * c, 2 * c + 1)):
-            block = dx_c[i * ROWS:(i + 1) * ROWS]
-            if d == 0:
-                rdx[0:ROWS] = block
-            else:
-                sdx[d * ROWS:(d + 1) * ROWS] = block
-                if c == 0:
-                    remote(3, sdx, rdx, d).start()
-
-    for c in range(4):
-        bwd_chunk(c)
+        sdx[rows] = dot_nt(da_v[rows], win_v[...]).astype(BF16)
+        return carry
+
+    lax.fori_loop(0, N_DEV // 2, bwd_chunk, 0)
+    rdx[0:ROWS] = sdx[0:ROWS]
     for d in DX_EARLY:
         remote(3, sdx, rdx, d).start()
 
@@ -217,7 +229,7 @@
     to_mate = wg_copy(0, wg_part.at[1 - core], wg_mate, 1)
     to_mate.start()
     out_ref[...] = (g0 * y0 + g1 * y1).astype(BF16)
-    acc = dot_nn(d_log, wgt_ref[...])
+    acc_ref[...] = dot_nn(d_log, wgt_ref[...])
     to_mate.wait_recv()
     wg_chip[chip] = wg_part[core] + wg_mate[...]
     to_chips = [wg_copy(1 + i, wg_chip.at[chip], wg_chip.at[chip], 2 * (i + 1)) for i in range(3)]
@@ -226,15 +238,6 @@
     for d in DX_LATE:
         remote(3, sdx, rdx, d).start()
 
-    for c in (0, 3):
-        for d in (2 * c, 2 * c + 1):
-            if d:
-                remote(3, sdx, rdx, d).wait_recv()
-        span = slice(2 * ROWS * c, 2 * ROWS * (c + 1))
-        acc = acc + dot_nn(q0_v[:, span] + q1_v[:, span], rdx[span])
-    acc_ref[...] = acc
-    span = slice(2 * ROWS, 6 * ROWS)
-    qlast_ref[...] = q0_v[:, span] + q1_v[:, span]
     for cp in to_chips:
         cp.wait_recv()
     gwg_ref[core] = (wg_chip[0] + wg_chip[1]) + (wg_chip[2] + wg_chip[3])
@@ -248,13 +251,11 @@
     for cp in to_chips:
         cp.wait_send()
     swap.wait()
-    for d in (2, 4, 3, 5):
-        remote(3, sdx, rdx, d).wait_recv()
     for d in range(1, N_DEV):
-        remote(3, sdx, rdx, d).wait_send()
-
-
-def finish_kernel(out_v, gwin_v, gwout_v, gwg_v, acc_v, qlast_v, dx_v,
+        remote(3, sdx, rdx, d).wait()
+
+
+def finish_kernel(out_v, gwin_v, gwout_v, gwg_v, acc_v, q01_v, dx_v,
                   out_hbm, gx_hbm, gwin_hbm, gwout_hbm, gwg_hbm, gx_v, sem):
     half = gwg_v.shape[2]
     pieces = [(gwin_v, gwin_hbm), (gwout_v, gwout_hbm), (out_v, out_hbm), (gwg_v.at[0], gwg_hbm.at[:, pl.ds(0, half)]),
@@ -262,7 +263,7 @@
     stores = [pltpu.make_async_copy(src, dst, sem.at[i]) for i, (src, dst) in enumerate(pieces)]
     for st in stores[:-1]:
         st.start()
-    gx_v[...] = (acc_v[...] + dot_nn(qlast_v[...], dx_v[2 * ROWS:6 * ROWS])).astype(BF16)
+    gx_v[...] = (acc_v[...] + dot_nn(q01_v[...], dx_v[...])).astype(BF16)
     stores[-1].start()
     for st in stores:
         st.wait()
@@ -282,7 +283,7 @@
         moe_kernel,
         out_shape=(pltpu.VMEM((tok, d_model), BF16), pltpu.VMEM((d_model, d_hid), F32), pltpu.VMEM((d_hid, d_model), F32),
                    pltpu.VMEM((2, n_exp, d_model // 2), F32), pltpu.VMEM((tok, d_model), F32),
-                   pltpu.VMEM((tok, 4 * ROWS), BF16), pltpu.VMEM((slots, d_model), BF16)),
+                   pltpu.VMEM((tok, slots), BF16), pltpu.VMEM((slots, d_model), BF16)),
         in_specs=[hbm] * 6,
         out_specs=(vmem,) * 7,
         scratch_shapes=[
@@ -294,7 +295,7 @@
             pltpu.VMEM((2 * tok, d_model), BF16), pltpu.VMEM((2, tok, 1), F32), pltpu.VMEM((tok, 128), F32),
             blocks, blocks, blocks, blocks, blocks, blocks, blocks,
             pltpu.VMEM((slots, d_hid), BF16), pltpu.VMEM((slots, d_hid), F32), pltpu.VMEM((slots, d_hid), BF16),
-            pltpu.VMEM((d_model, slots), BF16), pltpu.VMEM((tok, tok), BF16),
+            pltpu.VMEM((d_model, slots), BF16), pltpu.VMEM((ROWS, 2 * ROWS), BF16),
             pltpu.VMEM((2, n_exp, d_model // 2), F32), pltpu.VMEM((n_exp, d_model // 2), F32), pltpu.VMEM((4, n_exp, d_model // 2), F32),
             pltpu.SemaphoreType.DMA((6,)), pltpu.SemaphoreType.DMA((4, n_exp)), pltpu.SemaphoreType.DMA((4, n_exp)),
             pltpu.SemaphoreType.DMA((5,)), pltpu.SemaphoreType.DMA((5,)),

time: 56.5 us -> 56.1 us (level)
  no operation moved by 1% of the time
where the time goes in v5:
time: 56.1 us; the launch traced here: 55.9 us
  Pallas kernels  55.2 us (98%)
  between operations  0.64 us (1%)
    pallas_call x1, Pallas kernels, local_block(): pl.pallas_call(moe_kernel, out_shape=(pltpu.VMEM((tok, d_model), BF16), p...  51.6 us
    pallas_call x1, Pallas kernels, local_block(): pl.pallas_call(finish_kernel, out_shape=(jax.ShapeDtypeStruct((tok, d_mod...  3.67 us

profile of v5, /device:TPU:0, one launch (start us, length us, event | category | flops | bytes accessed | tf_op | source)
XLA Modules:
  0.0 55.9 jit_solution(11098894972023593909)
XLA Ops:
  0.6 51.6 %moe_step.1 = (bf16[512,512]{1,0:T(8,128)(2,1)S(1)}, f32[512,2048]{1,0:T(8,128)S(1)}, f32[2048,512]{1,0:T(8,128)S(1)}, f32[2,8,256]{2,1,0:T(8,128)S(1)}, f32[512...) custom-call(s32[2,512]{1,0:T(2,128)} %bitcast.10, bf16[8,512]{1,0:T(8,128)(2,1)} %bitcast.9, ...), custom_call_target="tpu_custom_call" | custom-call | tf_op jit(solution)/shard_map/moe_step/pallas_call | solution.py:282
  52.2 3.7 %moe_finish.1 = (bf16[512,512]{1,0:T(8,128)(2,1)}, bf16[512,512]{1,0:T(8,128)(2,1)}, f32[512,2048]{1,0:T(8,128)}, f32[2048,512]{1,0:T(8,128)}, f32[8,512]{1,0:T(8,128)}) custom-call(bf16[512,512]{1,0:T(8,128)(2,1)S(1)} %get-tuple-element.17.out_v, f32[512,2048]{1,0:T(8,128)S(1)} %get-tuple-element.18.gwin_v, f32[2048,512]{1,0:T(8,128)S(1)} %get-tuple-element.19.gwout_v, ...), custom_call_target="tpu_custom_call" | custom-call | tf_op jit(solution)/shard_map/moe_finish/pallas_call | solution.py:306

commit v6 on v5

--- a/solution.py
+++ b/solution.py
@@ -8,8 +8,8 @@
 from jax.sharding import PartitionSpec as P
 
 N_DEV = 8
-DX_EARLY = (1, 2, 4, 6, 3, 5)
-DX_LATE = (7,)
+DX_EARLY = (1, 2, 4, 6, 3)
+DX_LATE = (7, 5)
 ROWS = 128
 MESH = pl.DeviceIdType.MESH
 F32 = jnp.float32
@@ -32,7 +32,7 @@
 
 def moe_kernel(ids_hbm, wgt_hbm, x_hbm, dout_hbm, win_hbm, wout_hbm,
                out_ref, gwin_ref, gwout_ref, gwg_ref, acc_ref, q01_ref, rdx,
-               ids_ref, wgt_ref, x_v, dout_v, win_v, wout_v, rank_v, p_v, q0_v, q1_v, dyflat_v, gate_v, cols_v,
+               ids_ref, wgt_ref, x_v, dout_v, win_v, wout_v, rank_v, q0_v, q1_v, dyflat_v, gate_v, cols_v,
                sx, rx, sdy, rdy, sy, ry, sdx, h_v, gp_v, da_v, xt_v, before_v, wg_part, wg_mate, wg_chip,
                load_sem, send_sem, recv_sem, wg_send, wg_recv):
     tok = x_v.shape[0]
@@ -77,14 +77,14 @@
     rank = jnp.concatenate(rank, axis=1)
     rank0 = jnp.where(hit0, rank, -1.0)
     rank1 = jnp.where(hit1, rank, -1.0)
+    rank_v[32:48, :] = jnp.where(hit0 | hit1, rank, -1.0)
     rank_v[0:16, :] = rank0
     rank_v[16:32, :] = rank1
 
     loads[1].wait()
-    for d in (2, 4, 3, 5, 6, 7, 1, 0):
-        pick0 = jnp.where(rank_v[d:d + 1, :] == slot, 1.0, 0.0)
-        pick1 = jnp.where(rank_v[16 + d:17 + d, :] == slot, 1.0, 0.0)
-        block = dot_nn((pick0 + pick1).astype(BF16), x_v[...]).astype(BF16)
+    for d in (2, 4, 6, 3, 5, 7, 1, 0):
+        pick = jnp.where(rank_v[32 + d:33 + d, :] == slot, 1.0, 0.0).astype(BF16)
+        block = dot_nn(pick, x_v[...]).astype(BF16)
         if d == 0:
             rx[0:ROWS] = block
         else:
@@ -92,8 +92,6 @@
             if d == 2:
                 pl.semaphore_wait(barrier, N_DEV - 1)
             remote(0, sx, rx, d).start()
-        p_v[d, :, 0:tok] = pick0.astype(BF16)
-        p_v[d, :, tok:2 * tok] = pick1.astype(BF16)
 
     stack = jnp.concatenate([rank0, rank1, jnp.broadcast_to(ids0.astype(F32), (16, tok)),
                              jnp.broadcast_to(ids1.astype(F32), (16, tok)), jnp.zeros((64, tok), F32)], axis=0)
@@ -113,7 +111,9 @@
     dyflat_v[0:tok, :] = (gate_v[0] * dout_f).astype(BF16)
     dyflat_v[tok:2 * tok, :] = (gate_v[1] * dout_f).astype(BF16)
     for d in (2, 4, 3, 5, 6, 7, 1, 0):
-        block = dot_nn(p_v[d], dyflat_v[...]).astype(BF16)
+        pick0 = jnp.where(rank_v[d:d + 1, :] == slot, 1.0, 0.0).astype(BF16)
+        pick1 = jnp.where(rank_v[16 + d:17 + d, :] == slot, 1.0, 0.0).astype(BF16)
+        block = (dot_nn(pick0, dyflat_v[0:tok]) + dot_nn(pick1, dyflat_v[tok:2 * tok])).astype(BF16)
         if d == 0:
             rdy[0:ROWS] = block
         else:
@@ -290,7 +290,7 @@
             pltpu.VMEM((2, tok), jnp.int32), pltpu.VMEM((n_exp, d_model), BF16),
             pltpu.VMEM((tok, d_model), BF16), pltpu.VMEM((tok, d_model), BF16),
             pltpu.VMEM((d_model, d_hid), BF16), pltpu.VMEM((d_hid, d_model), BF16),
-            pltpu.VMEM((32, tok), F32), pltpu.VMEM((n_exp, ROWS, 2 * tok), BF16),
+            pltpu.VMEM((48, tok), F32),
             pltpu.VMEM((tok, slots), BF16), pltpu.VMEM((tok, slots), BF16),
             pltpu.VMEM((2 * tok, d_model), BF16), pltpu.VMEM((2, tok, 1), F32), pltpu.VMEM((tok, 128), F32),
             blocks, blocks, blocks, blocks, blocks, blocks, blocks,

time: 56.1 us -> 56 us (level)
  no operation moved by 1% of the time
where the time goes in v6:
time: 56 us; the launch traced here: 55.8 us
  Pallas kernels  55.2 us (99%)
  between operations  0.64 us (1%)
    pallas_call x1, Pallas kernels, local_block(): pl.pallas_call(moe_kernel, out_shape=(pltpu.VMEM((tok, d_model), BF16), p...  51.5 us
    pallas_call x1, Pallas kernels, local_block(): pl.pallas_call(finish_kernel, out_shape=(jax.ShapeDtypeStruct((tok, d_mod...  3.67 us

profile of v6, /device:TPU:0, one launch (start us, length us, event | category | flops | bytes accessed | tf_op | source)
XLA Modules:
  0.0 55.8 jit_solution(4297209555088737473)
XLA Ops:
  0.6 51.5 %moe_step.1 = (bf16[512,512]{1,0:T(8,128)(2,1)S(1)}, f32[512,2048]{1,0:T(8,128)S(1)}, f32[2048,512]{1,0:T(8,128)S(1)}, f32[2,8,256]{2,1,0:T(8,128)S(1)}, f32[512...) custom-call(s32[2,512]{1,0:T(2,128)} %bitcast.10, bf16[8,512]{1,0:T(8,128)(2,1)} %bitcast.9, ...), custom_call_target="tpu_custom_call" | custom-call | tf_op jit(solution)/shard_map/moe_step/pallas_call | solution.py:282
  52.2 3.7 %moe_finish.1 = (bf16[512,512]{1,0:T(8,128)(2,1)}, bf16[512,512]{1,0:T(8,128)(2,1)}, f32[512,2048]{1,0:T(8,128)}, f32[2048,512]{1,0:T(8,128)}, f32[8,512]{1,0:T(8,128)}) custom-call(bf16[512,512]{1,0:T(8,128)(2,1)S(1)} %get-tuple-element.17.out_v, f32[512,2048]{1,0:T(8,128)S(1)} %get-tuple-element.18.gwin_v, f32[2048,512]{1,0:T(8,128)S(1)} %get-tuple-element.19.gwout_v, ...), custom_call_target="tpu_custom_call" | custom-call | tf_op jit(solution)/shard_map/moe_finish/pallas_call | solution.py:306

commit v7 on v6

--- a/solution.py
+++ b/solution.py
@@ -82,16 +82,18 @@
     rank_v[16:32, :] = rank1
 
     loads[1].wait()
-    for d in (2, 4, 6, 3, 5, 7, 1, 0):
-        pick = jnp.where(rank_v[32 + d:33 + d, :] == slot, 1.0, 0.0).astype(BF16)
-        block = dot_nn(pick, x_v[...]).astype(BF16)
-        if d == 0:
-            rx[0:ROWS] = block
-        else:
-            sx[d * ROWS:(d + 1) * ROWS] = block
-            if d == 2:
-                pl.semaphore_wait(barrier, N_DEV - 1)
-            remote(0, sx, rx, d).start()
+    for group in ((2,), (4, 6), (3, 5), (7, 1), (0,)):
+        pick = jnp.concatenate([jnp.where(rank_v[32 + d:33 + d, :] == slot, 1.0, 0.0).astype(BF16) for d in group], axis=0)
+        blocks = dot_nn(pick, x_v[...]).astype(BF16)
+        for i, d in enumerate(group):
+            block = blocks[i * ROWS:(i + 1) * ROWS]
+            if d == 0:
+                rx[0:ROWS] = block
+            else:
+                sx[d * ROWS:(d + 1) * ROWS] = block
+                if d == 2:
+                    pl.semaphore_wait(barrier, N_DEV - 1)
+                remote(0, sx, rx, d).start()
 
     stack = jnp.concatenate([rank0, rank1, jnp.broadcast_to(ids0.astype(F32), (16, tok)),
                              jnp.broadcast_to(ids1.astype(F32), (16, tok)), jnp.zeros((64, tok), F32)], axis=0)

time: 56 us -> 56 us (level)
  no operation moved by 1% of the time
where the time goes in v7:
time: 56 us; the launch traced here: 55.8 us
  Pallas kernels  55.2 us (99%)
  between operations  0.64 us (1%)
    pallas_call x1, Pallas kernels, local_block(): pl.pallas_call(moe_kernel, out_shape=(pltpu.VMEM((tok, d_model), BF16), p...  51.5 us
    pallas_call x1, Pallas kernels, local_block(): pl.pallas_call(finish_kernel, out_shape=(jax.ShapeDtypeStruct((tok, d_mod...  3.67 us

profile of v7, /device:TPU:0, one launch (start us, length us, event | category | flops | bytes accessed | tf_op | source)
XLA Modules:
  0.0 55.8 jit_solution(16165361288757090969)
XLA Ops:
  0.6 51.5 %moe_step.1 = (bf16[512,512]{1,0:T(8,128)(2,1)S(1)}, f32[512,2048]{1,0:T(8,128)S(1)}, f32[2048,512]{1,0:T(8,128)S(1)}, f32[2,8,256]{2,1,0:T(8,128)S(1)}, f32[512...) custom-call(s32[2,512]{1,0:T(2,128)} %bitcast.10, bf16[8,512]{1,0:T(8,128)(2,1)} %bitcast.9, ...), custom_call_target="tpu_custom_call" | custom-call | tf_op jit(solution)/shard_map/moe_step/pallas_call | solution.py:284
  52.2 3.7 %moe_finish.1 = (bf16[512,512]{1,0:T(8,128)(2,1)}, bf16[512,512]{1,0:T(8,128)(2,1)}, f32[512,2048]{1,0:T(8,128)}, f32[2048,512]{1,0:T(8,128)}, f32[8,512]{1,0:T(8,128)}) custom-call(bf16[512,512]{1,0:T(8,128)(2,1)S(1)} %get-tuple-element.17.out_v, f32[512,2048]{1,0:T(8,128)S(1)} %get-tuple-element.18.gwin_v, f32[2048,512]{1,0:T(8,128)S(1)} %get-tuple-element.19.gwout_v, ...), custom_call_target="tpu_custom_call" | custom-call | tf_op jit(solution)/shard_map/moe_finish/pallas_call | solution.py:308

commit v8 on v7

--- a/solution.py
+++ b/solution.py
@@ -49,12 +49,14 @@
             src_ref=src.at[pl.ds(d * ROWS, ROWS)], dst_ref=dst.at[pl.ds(d * ROWS, ROWS)], send_sem=send_sem.at[phase, d], recv_sem=recv_sem.at[phase, d],
             device_id=(peer(d),), device_id_type=MESH)
 
+    loads = [pltpu.make_async_copy(src, dst, load_sem.at[i]) for i, (src, dst) in enumerate(
+        ((ids_hbm, ids_ref), (x_hbm, x_v), (wgt_hbm, wgt_ref), (dout_hbm, dout_v), (win_hbm, win_v), (wout_hbm, wout_v)))]
+    for ld in loads[:2]:
+        ld.start()
     barrier = pltpu.get_barrier_semaphore()
     for d in range(1, N_DEV):
         pl.semaphore_signal(barrier, inc=1, device_id=(peer(d),), device_id_type=MESH)
-    loads = [pltpu.make_async_copy(src, dst, load_sem.at[i]) for i, (src, dst) in enumerate(
-        ((ids_hbm, ids_ref), (x_hbm, x_v), (wgt_hbm, wgt_ref), (dout_hbm, dout_v), (win_hbm, win_v), (wout_hbm, wout_v)))]
-    for ld in loads:
+    for ld in loads[2:]:
         ld.start()
 
     rel = lax.broadcasted_iota(jnp.int32, (16, tok), 0) ^ me

time: 56 us -> 55.9 us (level)
  no operation moved by 1% of the time
where the time goes in v8:
time: 55.9 us; the launch traced here: 55.8 us
  Pallas kernels  55.1 us (99%)
  between operations  0.64 us (1%)
    pallas_call x1, Pallas kernels, local_block(): pl.pallas_call(moe_kernel, out_shape=(pltpu.VMEM((tok, d_model), BF16), p...  51.5 us
    pallas_call x1, Pallas kernels, local_block(): pl.pallas_call(finish_kernel, out_shape=(jax.ShapeDtypeStruct((tok, d_mod...  3.67 us

profile of v8, /device:TPU:0, one launch (start us, length us, event | category | flops | bytes accessed | tf_op | source)
XLA Modules:
  0.0 55.8 jit_solution(4556034758010524324)
XLA Ops:
  0.6 51.5 %moe_step.1 = (bf16[512,512]{1,0:T(8,128)(2,1)S(1)}, f32[512,2048]{1,0:T(8,128)S(1)}, f32[2048,512]{1,0:T(8,128)S(1)}, f32[2,8,256]{2,1,0:T(8,128)S(1)}, f32[512...) custom-call(s32[2,512]{1,0:T(2,128)} %bitcast.10, bf16[8,512]{1,0:T(8,128)(2,1)} %bitcast.9, ...), custom_call_target="tpu_custom_call" | custom-call | tf_op jit(solution)/shard_map/moe_step/pallas_call | solution.py:286
  52.1 3.7 %moe_finish.1 = (bf16[512,512]{1,0:T(8,128)(2,1)}, bf16[512,512]{1,0:T(8,128)(2,1)}, f32[512,2048]{1,0:T(8,128)}, f32[2048,512]{1,0:T(8,128)}, f32[8,512]{1,0:T(8,128)}) custom-call(bf16[512,512]{1,0:T(8,128)(2,1)S(1)} %get-tuple-element.17.out_v, f32[512,2048]{1,0:T(8,128)S(1)} %get-tuple-element.18.gwin_v, f32[2048,512]{1,0:T(8,128)S(1)} %get-tuple-element.19.gwout_v, ...), custom_call_target="tpu_custom_call" | custom-call | tf_op jit(solution)/shard_map/moe_finish/pallas_call | solution.py:310
